TPU v7x, 256 devices: a whole 4x4x8 slice. The times are simulated.
256 devices in a mesh: row: 8 (over x, core), col: 32 (over z, y).
Axes of the slice: x: 4, y: 4, z: 8, core: 2. Of those that a mesh axis runs over, the one named last changes fastest.
Arguments:
- trailing: float32 [16384, 16384], P('row', 'col'), may hold values from -9 to 9
- panel: float32 [16384, 256], P('row'), may hold values from -21 to 21
Outputs:
- updated: float32 [16384, 16384], P('row', 'col')
- band: float32 [256, 256], replicated
All inputs are finite; a program needn't handle non-finite values.
Results may differ from a plain program's by a relative error of at most 0.0003.
Values sent between devices are 32-bit elements; how exact they have to be, the bound alone decides.
No kernel may reach another device: no remote copies, remote signals or barrier semaphores. Data moves between devices by JAX's collectives and lax.ppermute only.
A program may use at most 128 MiB of HBM per device.

v0:
```python
import functools

import jax
import jax.numpy as jnp
from jax import lax
from jax.experimental import pallas as pl
from jax.experimental.pallas import tpu as pltpu
from jax.sharding import Mesh
from jax.sharding import PartitionSpec as P

ALL = ("x", "core", "z", "y")
NB = 64
WINDOW = 8
WINDOW_FULL = 6
STEPS = 4
HIGHEST = lax.Precision.HIGHEST
HIGH = lax.Precision.HIGH


def dot(left, right, dims, precision):
    return lax.dot_general(
        left, right, (dims, ((), ())), precision=precision, preferred_element_type=jnp.float32
    )


def nn(left, right, precision=HIGHEST):
    return dot(left, right, ((1,), (0,)), precision)


def nt(left, right, precision=HIGHEST):
    return dot(left, right, ((1,), (1,)), precision)


def tn(left, right, precision=HIGHEST):
    return dot(left, right, ((0,), (0,)), precision)


def unit_eye(n):
    rows = lax.broadcasted_iota(jnp.int32, (n, n), 0)
    cols = lax.broadcasted_iota(jnp.int32, (n, n), 1)
    return (rows == cols).astype(jnp.float32)


def at_block(k, value, size):
    found = value[:, :size]
    for j in range(1, value.shape[1] // size):
        found = jnp.where(k == j, value[:, j * size : (j + 1) * size], found)
    return found


def eliminate(block, full):
    count = NB // 8
    window = WINDOW_FULL if full else WINDOW
    aug = jnp.concatenate([block, unit_eye(NB)], axis=1)
    wide = aug.shape[1]
    tiles = [aug[8 * i : 8 * i + 8] for i in range(count)]
    sub = lax.broadcasted_iota(jnp.int32, (8, wide), 0)

    def spread(j, now):
        first = 0 if full else now // 8
        return {i: jnp.broadcast_to(tiles[i][:, j : j + 1], (8, wide)) for i in range(first, count)}

    def line(tile, s):
        return jnp.broadcast_to(tile[s : s + 1], (8, wide))

    ahead = {j: spread(j, 0) for j in range(min(window, NB))}
    for j in range(NB):
        t, s = divmod(j, 8)
        mine = ahead.pop(j)
        inverse = 1.0 / line(mine[t], s)
        where = range(0 if full else t, count)
        factor = {i: mine[i] * inverse for i in where}
        factor[t] = jnp.where(sub != s if full else sub > s, factor[t], 0.0)
        scale = jnp.where(sub == s, inverse, 1.0) if full else None

        def step(tile, i, pivot):
            kept = tile * scale if full and i == t else tile
            return kept - factor[i] * pivot

        pivot = line(tiles[t], s)
        for i in where:
            tiles[i] = step(tiles[i], i, pivot)
        for l in sorted(ahead):
            pivot = line(ahead[l][t], s)
            ahead[l] = {i: step(ahead[l][i], i, pivot) for i in ahead[l] if i in where}
        if j + window < NB:
            ahead[j + window] = spread(j + window, j + 1)
    return jnp.concatenate(tiles, axis=0)


def halves(value):
    high = value.astype(jnp.bfloat16)
    return high, (value - high.astype(jnp.float32)).astype(jnp.bfloat16)


def thirds(value):
    high, rest = halves(value)
    low = value - high.astype(jnp.float32) - rest.astype(jnp.float32)
    return high, rest, low.astype(jnp.bfloat16)


def one(left, right, dims):
    return dot(left, right, dims, lax.Precision.DEFAULT)


def dot3(left, right, dims):
    (lh, ll), (rh, rl) = left, right
    (ld,), (rd,) = dims
    return one(jnp.concatenate([lh, lh, ll], axis=ld), jnp.concatenate([rh, rl, rh], axis=rd), dims)


def share_out(core, value, lanes, kept_ref, sent_ref):
    chips, rows, _ = kept_ref.shape
    for q in range(chips):
        for ref, side in ((kept_ref, core), (sent_ref, 1 - core)):
            at = pl.multiple_of((2 * q + side) * rows, rows)
            ref[q, :, lanes] = value[pl.ds(at, rows), :]


def gram_kernel(place_ref, panel_ref, kept_ref, sent_ref, total, cross):
    width = panel_ref.shape[1]
    rows = panel_ref.shape[0] // STEPS
    dims = ((1,), (0,))
    total[...] = jnp.zeros_like(total)
    cross[...] = jnp.zeros_like(cross)

    @pl.loop(0, STEPS)
    def _(c):
        block = panel_ref[pl.ds(pl.multiple_of(c * rows, rows), rows), :]
        high, rest, low = thirds(block)
        high_t, rest_t = halves(block.T)
        total[...] += one(
            jnp.concatenate([high_t, rest_t], axis=1), jnp.concatenate([high, rest], axis=0), dims
        )
        cross[...] += one(
            jnp.concatenate([high_t, high_t], axis=1), jnp.concatenate([rest, low], axis=0), dims
        )

    total[...] = total[...] + (cross[...] + cross[...].T)
    core = place_ref[1]
    first = (place_ref[0] + core == 0).astype(jnp.float32)
    cross[...] = panel_ref[:width] * first
    share_out(core, total, slice(0, width), kept_ref, sent_ref)
    share_out(core, cross, slice(width, 2 * width), kept_ref, sent_ref)


def product_kernel(place_ref, trailing_ref, panel_ref, kept_ref, sent_ref, total, edge):
    width = panel_ref.shape[1]
    rows = panel_ref.shape[0] // STEPS
    core = place_ref[1]
    first = (place_ref[0] + core == 0).astype(jnp.float32)
    edge[...] = trailing_ref[:width].T * first
    total[...] = jnp.zeros_like(total)

    @pl.loop(0, STEPS)
    def _(c):
        at = pl.ds(pl.multiple_of(c * rows, rows), rows)
        total[...] += dot3(halves(trailing_ref[at, :].T), halves(panel_ref[at, :]), ((1,), (0,)))

    share_out(core, total, slice(0, width), kept_ref, sent_ref)
    share_out(core, edge, slice(width, 2 * width), kept_ref, sent_ref)


def stream_call(kernel, place, arrays, out, scratch, flops):
    vmem = pl.BlockSpec(memory_space=pltpu.VMEM)
    return pl.pallas_call(
        kernel,
        out_shape=[jax.ShapeDtypeStruct(out, jnp.float32)] * 2,
        in_specs=[pl.BlockSpec(memory_space=pltpu.SMEM)] + [vmem] * len(arrays),
        out_specs=[vmem] * 2,
        scratch_shapes=[pltpu.VMEM(s, jnp.float32) for s in scratch],
        compiler_params=pltpu.CompilerParams(vmem_limit_bytes=24 * 2**20),
        cost_estimate=estimate(flops),
    )(place, *arrays)


def factor_kernel(place_ref, sums_ref, other_ref, band_ref, inv_ref, sign_ref, top_ref, work, whole):
    width = band_ref.shape[0]
    ring, thin, _ = sums_ref.shape
    x, core = place_ref[0], place_ref[1]
    for s in range(ring):
        base = lax.rem(x + ring - s, ring) * (2 * thin)
        whole[pl.ds(pl.multiple_of(base + core * thin, thin), thin), :] = sums_ref[s]
        whole[pl.ds(pl.multiple_of(base + (1 - core) * thin, thin), thin), :] = other_ref[s]
    work[:, :width] = whole[:, :width]
    work[:, width:] = unit_eye(width)
    top_ref[...] = whole[:, width:]
    for k in range(width // NB):
        lo, hi = k * NB, (k + 1) * NB
        done = eliminate(work[lo:hi, lo:hi], False)
        diag = jnp.sum(done[:, :NB] * unit_eye(NB), axis=1, keepdims=True)
        low = done[:, NB:] * lax.rsqrt(diag)
        right = width + hi
        rows = nn(low, work[lo:hi, lo:right])
        work[lo:hi, lo:right] = rows
        if hi < width:
            work[hi:, hi:right] = work[hi:, hi:right] - tn(rows[:, NB : width - lo], rows[:, NB:])

    eye_r = lax.broadcasted_iota(jnp.int32, (width, width), 0)
    eye_c = lax.broadcasted_iota(jnp.int32, (width, width), 1)
    upper = jnp.where(eye_r <= eye_c, work[:, :width], 0.0)
    inv = jnp.where(eye_r >= eye_c, work[:, width:], 0.0)
    diag_q = jnp.sum(top_ref[...] * inv, axis=1, keepdims=True)
    signs = jnp.where(diag_q > 0.0, -1.0, jnp.where(diag_q < 0.0, 1.0, 0.0))
    band_ref[...] = signs * upper
    inv_ref[...] = inv
    row = jnp.sum(jnp.where(eye_r == eye_c, signs, 0.0), axis=0, keepdims=True)
    sign_ref[...] = jnp.broadcast_to(row, sign_ref.shape)


def block_kernel(top_ref, inv_ref, sign_ref, out_ref, work, side):
    width = top_ref.shape[0]
    work[:, :width] = unit_eye(width) - nt(inv_ref[...], top_ref[...]) * sign_ref[0:1, :]
    work[:, width:] = unit_eye(width)
    index = lax.broadcasted_iota(jnp.int32, (width, 1), 0)

    @pl.loop(0, width // NB)
    def _(k):
        lo = pl.multiple_of(k * NB, NB)
        cols = at_block(k, work[:, :width], NB)
        side[...] = cols
        done = eliminate(side[pl.ds(lo, NB), :], True)
        rows = nn(done[:, NB:], work[pl.ds(lo, NB), :])
        cols = jnp.where((index >= lo) & (index < lo + NB), 0.0, cols)
        work[...] = work[...] - dot3(halves(cols), halves(rows), ((1,), (0,)))
        work[pl.ds(lo, NB), :] = rows

    out_ref[...] = work[:, width:]


def right_kernel(
    place_ref, cols_ref, other_ref, block_ref, coupling_ref, right_ref, whole
):
    width = block_ref.shape[0]
    ring, piece, _ = cols_ref.shape
    x, core = place_ref[0], place_ref[1]
    for s in range(ring):
        base = lax.rem(x + ring - s, ring) * (2 * piece)
        whole[pl.ds(pl.multiple_of(base + core * piece, piece), piece), :] = cols_ref[s]
        whole[pl.ds(pl.multiple_of(base + (1 - core) * piece, piece), piece), :] = other_ref[s]
    block = halves(block_ref[...])
    x_cols, y_cols = halves(whole[:, :width]), halves(whole[:, width:])
    w = dot3(x_cols, block, ((1,), (0,)))
    w = w - dot3(y_cols, halves(coupling_ref[...]), ((1,), (0,)))
    d = dot3(y_cols, block, ((1,), (1,)))
    high, low = halves(jnp.concatenate([w, d], axis=1).T)
    span = high.shape[0]
    right_ref[:span] = high
    right_ref[span : 2 * span] = low
    right_ref[2 * span :] = high


def update_kernel(
    place_ref, trailing_ref, y_ref, own_ref, up_ref, over_ref, down_ref, right_ref,
    out_ref, tile, result, left, semaphores, done,
):
    count, width = own_ref.shape
    sources = (own_ref, up_ref, over_ref, down_ref)

    def rows_of(step):
        to = lax.rem(place_ref[2] + len(sources) - step, len(sources))
        return pl.ds(pl.multiple_of(to * count, count), count)

    def loading(step):
        return pltpu.make_async_copy(
            trailing_ref.at[rows_of(step)], tile.at[step], semaphores.at[step]
        )

    def storing(step):
        return pltpu.make_async_copy(result.at[step], out_ref.at[rows_of(step)], done.at[step])

    for step in range(len(sources)):
        loading(step).start()

    @pl.loop(0, len(sources))
    def _(step):
        for n, source in enumerate(sources):

            @pl.when(step == n)
            def _():
                high, low = halves(source[...])
                left[:, width : 2 * width] = high
                left[:, 3 * width : 4 * width] = high
                left[:, 5 * width :] = low

        high, low = halves(y_ref[rows_of(step), :])
        left[:, :width] = high
        left[:, 2 * width : 3 * width] = high
        left[:, 4 * width : 5 * width] = low
        loading(step).wait()
        result[step] = tile[step] - one(left[...], right_ref[...], ((1,), (0,)))
        storing(step).start()

    for step in range(len(sources)):
        storing(step).wait()


def local_call(kernel, outs, scratch, *args, **more):
    return pl.pallas_call(
        kernel,
        out_shape=[jax.ShapeDtypeStruct(s, jnp.float32) for s in outs],
        scratch_shapes=[pltpu.VMEM(s, t) for s, t in scratch],
        compiler_params=pltpu.CompilerParams(vmem_limit_bytes=30 * 2**20),
        **more,
    )(*args)


def estimate(flops):
    return pl.CostEstimate(flops=flops, bytes_accessed=2**20, transcendentals=0)


def update_call(place, trailing, y_rows, sources, cols, cols_other, block, coupling):
    count, width = sources[0].shape
    y_n = len(sources)
    span = trailing.shape[1]
    tiles = (y_n, count, span)
    smem = pl.BlockSpec(memory_space=pltpu.SMEM)
    vmem = pl.BlockSpec(memory_space=pltpu.VMEM)
    hbm = pl.BlockSpec(memory_space=pltpu.HBM)
    right = pl.pallas_call(
        right_kernel,
        name="right_kernel",
        out_shape=jax.ShapeDtypeStruct((6 * width, span), jnp.bfloat16),
        in_specs=[smem] + [vmem] * 4,
        out_specs=vmem,
        scratch_shapes=[pltpu.VMEM((span, 2 * width), jnp.float32)],
        compiler_params=pltpu.CompilerParams(vmem_limit_bytes=30 * 2**20),
        cost_estimate=estimate(2 * 10**9),
    )(place, cols, cols_other, block, coupling)
    args = (y_rows, *sources, right)
    return pl.pallas_call(
        update_kernel,
        name="update_kernel",
        out_shape=jax.ShapeDtypeStruct(trailing.shape, jnp.float32),
        in_specs=[smem, hbm] + [vmem] * len(args),
        out_specs=hbm,
        scratch_shapes=[
            pltpu.VMEM(tiles, jnp.float32),
            pltpu.VMEM(tiles, jnp.float32),
            pltpu.VMEM((count, 6 * width), jnp.bfloat16),
            pltpu.SemaphoreType.DMA((y_n,)),
            pltpu.SemaphoreType.DMA((y_n,)),
        ],
        compiler_params=pltpu.CompilerParams(vmem_limit_bytes=30 * 2**20),
        cost_estimate=estimate(2 * 10**9),
    )(place, trailing, *args)


def exchange(x, axis):
    return lax.all_to_all(x, axis, 0, 0, tiled=True)


def to_everyone(x, axis):
    return exchange(jnp.broadcast_to(x[None], (lax.axis_size(axis), *x.shape)), axis)


def shift(x, axis, by):
    n = lax.axis_size(axis)
    return lax.ppermute(x, axis, [(i, (i + by) % n) for i in range(n)])


def around(x, axis):
    found = [x]
    for s in range(1, lax.axis_size(axis)):
        found.append(shift(x, axis, s))
    return found


def scatter_sum(parts, axis):
    n = lax.axis_size(axis)
    me = lax.axis_index(axis)
    total = lax.dynamic_index_in_dim(parts, me, 0, keepdims=False)
    for s in range(1, n):
        to = lax.dynamic_index_in_dim(parts, (me + s) % n, 0, keepdims=False)
        total = total + shift(to, axis, s)
    return total


def pair_sum(kept, sent):
    return kept + shift(sent, "core", 1)


def shards(trailing, panel):
    width = panel.shape[1]
    local_rows = panel.shape[0]
    local_cols = trailing.shape[1]
    x_n, core_n, z_n, y_n = (lax.axis_size(a) for a in ALL)
    x, core, z, y = (lax.axis_index(a) for a in ALL)
    row = x * core_n + core
    rows_n = x_n * core_n
    piece = local_cols // rows_n
    thin = width // rows_n
    first = (row == 0).astype(jnp.float32)
    swap = [
        ((r * z_n + c) * y_n + k, (c * z_n + r) * y_n + k)
        for r in range(rows_n)
        for c in range(z_n)
        for k in range(y_n)
    ]
    place = jnp.stack([x, core, y]).astype(jnp.int32)

    kept, sent = stream_call(
        gram_kernel,
        place,
        [panel],
        (x_n, thin, 2 * width),
        [(width, width)] * 2,
        10**9,
    )
    sums = jnp.stack(around(scatter_sum(pair_sum(kept, sent), "x"), "x"))
    other = shift(sums, "core", 1)

    kept, sent = stream_call(
        product_kernel,
        place,
        [trailing, panel],
        (x_n, piece, 2 * width),
        [(local_cols, width)] * 2,
        2 * 10**9,
    )
    pieces = scatter_sum(pair_sum(kept, sent), "x")
    mine = lax.dynamic_slice_in_dim(panel, y * local_cols, local_cols, 0)
    to_swap = lax.dynamic_slice_in_dim(panel, y * local_cols + z * piece, piece, 0)
    swapped = lax.ppermute(jnp.concatenate([pieces, to_swap], axis=1), ALL, swap)
    panel_piece = swapped[:, 2 * width :]

    smem = pl.BlockSpec(memory_space=pltpu.SMEM)
    vmem = pl.BlockSpec(memory_space=pltpu.VMEM)
    band, inv, sign, top = local_call(
        factor_kernel,
        [(width, width), (width, width), (8, width), (width, width)],
        [((width, 2 * width), jnp.float32)] * 2,
        place, sums, other,
        in_specs=[smem, vmem, vmem],
        cost_estimate=estimate(3 * 10**9),
    )
    (block,) = local_call(
        block_kernel,
        [(width, width)],
        [((width, 2 * width), jnp.float32), ((width, NB), jnp.float32)],
        top, inv, sign,
        cost_estimate=estimate(4 * 10**9),
    )
    sign = sign[0:1]

    def reflectors(rows_of_panel, is_first, count):
        at = lax.broadcasted_iota(jnp.int32, (count, width), 0)
        to = lax.broadcasted_iota(jnp.int32, (count, width), 1)
        return nt(rows_of_panel, inv, HIGH) - jnp.where(at + is_first == to, sign, 0.0)

    far = 2 * local_rows

    def products(both):
        return nt(both[:, :width], inv, HIGH) - both[:, width : 2 * width] * sign

    x_block = to_everyone(products(swapped), "z").reshape(local_cols, width)
    y_block = reflectors(mine, jnp.where(row == 0, y * local_cols, far), local_cols)
    y_rows = reflectors(panel, jnp.where(row == 0, 0, far), local_rows)
    y_piece = reflectors(
        panel_piece, jnp.where((z == 0) & (y == 0), row * piece, far), piece
    )
    cols = jnp.stack(around(jnp.concatenate([products(pieces), y_piece], axis=1), "x"))
    cols_other = shift(cols, "core", 1)

    x_block, block = lax.optimization_barrier((x_block, block))
    inner = tn(y_block, x_block)
    inner = lax.dynamic_slice_in_dim(inner, z * (width // z_n), width // z_n, 0)
    inner, x_block = lax.optimization_barrier((inner, x_block))
    for axis in ("y", "core", "x"):
        inner = functools.reduce(jnp.add, around(inner, axis))
    inner = to_everyone(inner, "z").reshape(width, width)
    coupling = tn(block, nn(inner, block))
    sources = around(x_block, "y")

    updated = update_call(place, trailing, y_rows, sources, cols, cols_other, block, coupling)
    return (updated, band)


def solution(mesh):
    finer = Mesh(mesh.devices.reshape(mesh.shape["row"] // 2, 2, 8, 4), ALL)
    placed = (P(("x", "core"), ("z", "y")), P(("x", "core"), None))
    return jax.shard_map(
        shards,
        mesh=finer,
        in_specs=placed,
        out_specs=(P(("x", "core"), ("z", "y")), P()),
        check_vma=False,
    )
```

profile of v0, /device:TPU:1, one launch (start us, length us, event | category | flops | bytes accessed | tf_op | source)
XLA Modules:
  0.0 148.5 jit_solution(1369405560144818310)
XLA Ops:
  0.7 1.6 %copy-done.2 = f32[2048,256]{1,0:T(8,128)S(1)} copy-done((f32[2048,256]{1,0:T(8,128)S(1)}, f32[2048,256]{1,0:T(8,128)}, u32[]{:S(2)}) %copy-start.2) | copy-done | bytes 2097176
  2.3 2.7 %shard_map.41 = (f32[4,32,512]{2,1,0:T(8,128)S(1)}, f32[4,32,512]{2,1,0:T(8,128)S(1)}) custom-call(s32[3]{0:T(128)S(1)} %pad_add_fusion.place_ref, f32[2048,256]{1,0:T(8,128)S(1)} %copy-done.2), custom_call_target="tpu_custom_call" | custom-call | flops 1000000000 | bytes 1048576 | tf_op jit(solution)/shard_map/pallas_call | solution.py:166
  5.0 3.3 %collective-permute-start = (f32[4,32,512]{2,1,0:T(8,128)S(1)}, f32[4,32,512]{2,1,0:T(8,128)S(1)}, u32[]{:S(2)}, u32[]{:S(2)}) collective-permute-start(f32[4,32,512]{2,1,0:T(8,128)S(1)} %get-tuple-element.15), channel_id=1, source_target_pairs={{0,32},{32,0},{1,33},{33,1},{2,34},{34,2},{3,35},{35,3},{4,36},{36... | collective-permute-start | bytes 786440 | tf_op jit(solution)/shard_map/ppermute | solution.py:359
  8.3 2.2 %copy-done = f32[2048,512]{1,0:T(8,128)S(1)} copy-done((f32[2048,512]{1,0:T(8,128)S(1)}, f32[2048,512]{1,0:T(8,128)}, u32[]{:S(2)}) %copy-start) | copy-done | bytes 4194328
  10.5 4.9 %shard_map.43 = (f32[4,64,512]{2,1,0:T(8,128)S(1)}, f32[4,64,512]{2,1,0:T(8,128)}) custom-call(s32[3]{0:T(128)S(1)} %pad_add_fusion.place_ref, f32[2048,512]{1,0:T(8,128)S(1)} %copy-done, f32[2048,256]{1,0:T(8,128)S(1)} %copy-done.3), custom_call_target="tpu_custom_call" | custom-call | flops 2000000000 | bytes 1048576 | tf_op jit(solution)/shard_map/pallas_call | solution.py:166
  15.5 2.7 %collective-permute-start.3 = (f32[32,512]{1,0:T(8,128)S(1)}, f32[32,512]{1,0:T(8,128)S(1)}, u32[]{:S(2)}, u32[]{:S(2)}) collective-permute-start(f32[32,512]{1,0:T(8,128)S(1)} %get-tuple-element.30), channel_id=1, source_target_pairs={{0,192},{64,0},{128,64},{192,128},{1,193},{65,1},{129,65},{193,129... | collective-permute-start | bytes 196616 | tf_op jit(solution)/shard_map/ppermute | solution.py:359
  18.2 1.6 %collective-permute-done.1 = f32[32,512]{1,0:T(8,128)S(1)} collective-permute-done((f32[32,512]{1,0:T(8,128)S(1)}, f32[32,512]{1,0:T(8,128)S(1)}, u32[]{:S(2)}, u32[]{:S(2)}) %collective-permute-start.1) | collective-permute-done | bytes 65568 | tf_op jit(solution)/shard_map/ppermute | solution.py:359
  20.1 2.7 %collective-permute-done.2 = f32[32,512]{1,0:T(8,128)S(1)} collective-permute-done((f32[32,512]{1,0:T(8,128)S(1)}, f32[32,512]{1,0:T(8,128)S(1)}, u32[]{:S(2)}, u32[]{:S(2)}) %collective-permute-start.2) | collective-permute-done | bytes 65568 | tf_op jit(solution)/shard_map/ppermute | solution.py:359
  22.8 1.7 %collective-permute-start.6 = (f32[32,512]{1,0:T(8,128)S(1)}, f32[32,512]{1,0:T(8,128)S(1)}, u32[]{:S(2)}, u32[]{:S(2)}) collective-permute-start(f32[32,512]{1,0:T(8,128)S(1)} %fusion.8), channel_id=1, source_target_pairs={{0,192},{64,0},{128,64},{192,128},{1,193},{65,1},{129,65},{193,129... | collective-permute-start | bytes 196616 | tf_op jit(solution)/shard_map/ppermute | solution.py:359
  25.2 1.9 %add.144 = f32[4,64,512]{2,1,0:T(8,128)} add(f32[4,64,512]{2,1,0:T(8,128)S(1)} %get-tuple-element.18, f32[4,64,512]{2,1,0:T(8,128)} %collective-permute-done.8) | non-fusion elementwise | flops 131072 | bytes 1572864 | tf_op jit(solution)/shard_map/add | solution.py:380
  27.1 1.1 dynamic-slice_bitcast_fusion.2
  28.1 2.0 %collective-permute-start.9 = (f32[64,512]{1,0:T(8,128)S(1)}, f32[64,512]{1,0:T(8,128)S(1)}, u32[]{:S(2)}, u32[]{:S(2)}) collective-permute-start(f32[64,512]{1,0:T(8,128)S(1)} %get-tuple-element.26), channel_id=1, source_target_pairs={{0,64},{64,128},{128,192},{192,0},{1,65},{65,129},{129,193},{193,1... | collective-permute-start | bytes 393224 | tf_op jit(solution)/shard_map/ppermute | solution.py:359
  30.2 0.7 collective-permute-start.11
  30.9 1.6 %collective-permute-start.10 = (f32[64,512]{1,0:T(8,128)S(1)}, f32[64,512]{1,0:T(8,128)S(1)}, u32[]{:S(2)}, u32[]{:S(2)}) collective-permute-start(f32[64,512]{1,0:T(8,128)S(1)} %get-tuple-element.28), channel_id=1, source_target_pairs={{0,128},{64,192},{128,0},{192,64},{1,129},{65,193},{129,1},{193,65... | collective-permute-start | bytes 393224 | tf_op jit(solution)/shard_map/ppermute | solution.py:359
  32.5 4.0 %collective-permute-start.7 = (f32[4,32,512]{2,1,0:T(8,128)S(1)}, f32[4,32,512]{2,1,0:T(8,128)S(1)}, u32[]{:S(2)}, u32[]{:S(2)}) collective-permute-start(f32[4,32,512]{2,1,0:T(8,128)S(1)} %pad_maximum_fusion.1.sums_ref), channel_id=1, source_target_pairs={{0,32},{32,0},{1,33},{33,1},{2,34},{34,2},{3,35},{35,3},{4,36},{36... | collective-permute-start | bytes 786440 | tf_op jit(solution)/shard_map/ppermute | solution.py:359
  36.5 0.8 collective-permute-done.10
  37.3 0.9 fusion.3
  38.2 5.7 %collective-permute-start.12 = (f32[64,768]{1,0:T(8,128)S(1)}, f32[64,768]{1,0:T(8,128)S(1)}, u32[]{:S(2)}, u32[]{:S(2)}) collective-permute-start(f32[64,768]{1,0:T(8,128)S(1)} %pad_maximum_fusion.2), channel_id=1, source_target_pairs={{0,0},{1,1},{2,2},{3,3},{4,32},{5,33},{6,34},{7,35},{8,64},{9,65},... | collective-permute-start | bytes 589832 | tf_op jit(solution)/shard_map/ppermute | solution.py:424
  44.0 10.6 %shard_map.42 = (f32[256,256]{1,0:T(8,128)}, f32[256,256]{1,0:T(8,128)S(1)}, f32[8,256]{1,0:T(8,128)S(1)}, f32[256,256]{1,0:T(8,128)S(1)}) custom-call(s32[3]{0:T(128)S(1)} %pad_add_fusion.place_ref, f32[4,32,512]{2,1,0:T(8,128)S(1)} %pad_maximum_fusion.1.sums_ref, f32[4,32,512]{2,1,0:T(8,128)S(1)} %collective-permute-done.7.other_ref), custom_call_target="tpu_custom_call" | custom-call | flops 3000000000 | bytes 1048576 | tf_op jit(solution)/shard_map/pallas_call | solution.py:299
  55.5 0.8 broadcast_in_dim.53
  56.4 6.6 %all-to-all-start = ((f32[8,64,256]{2,1,0:T(8,128)}), f32[8,64,256]{2,1,0:T(8,128)S(1)}, u32[]{:S(2)}, u32[]{:S(2)}) async-start(f32[8,64,256]{2,1,0:T(8,128)} %broadcast_in_dim.53), calls=%async_computation | async-start | bytes 1048576 | tf_op jit(solution)/shard_map/all_to_all | solution.py:350
  64.1 1.2 convolution_subtract_fusion
  65.3 11.6 %shard_map.44.block_ref = f32[256,256]{1,0:T(8,128)S(1)} custom-call(f32[256,256]{1,0:T(8,128)S(1)} %get-tuple-element.20.top_ref, f32[256,256]{1,0:T(8,128)S(1)} %get-tuple-element.16.inv_ref, f32[8,256]{1,0:T(8,128)S(1)} %get-tuple-element.17.sign_ref), custom_call_target="tpu_custom_call" | custom-call | flops 4000000000 | bytes 1048576 | tf_op jit(solution)/shard_map/pallas_call | solution.py:299
  77.0 1.0 fusion.11
  78.0 2.8 %collective-permute-start.22 = (f32[32,256]{1,0:T(8,128)S(1)}, f32[32,256]{1,0:T(8,128)S(1)}, u32[]{:S(2)}, u32[]{:S(2)}) collective-permute-start(f32[32,256]{1,0:T(8,128)S(1)} %constant_dynamic-slice_fusion), channel_id=1, source_target_pairs={{0,3},{1,0},{2,1},{3,2},{4,7},{5,4},{6,5},{7,6},{8,11},{9,8},{10,9... | collective-permute-start | bytes 98312 | tf_op jit(solution)/shard_map/ppermute | solution.py:359
  81.2 0.7 collective-permute-start.20
  82.1 3.0 %collective-permute-done.21 = f32[32,256]{1,0:T(8,128)S(1)} collective-permute-done((f32[32,256]{1,0:T(8,128)S(1)}, f32[32,256]{1,0:T(8,128)S(1)}, u32[]{:S(2)}, u32[]{:S(2)}) %collective-permute-start.21) | collective-permute-done | bytes 32800 | tf_op jit(solution)/shard_map/ppermute | solution.py:359
  85.4 6.3 %collective-permute-start.23 = (f32[32,256]{1,0:T(8,128)S(1)}, f32[32,256]{1,0:T(8,128)S(1)}, u32[]{:S(2)}, u32[]{:S(2)}) collective-permute-start(f32[32,256]{1,0:T(8,128)S(1)} %add_add_fusion.1), channel_id=1, source_target_pairs={{0,32},{32,0},{1,33},{33,1},{2,34},{34,2},{3,35},{35,3},{4,36},{36... | collective-permute-start | bytes 98312 | tf_op jit(solution)/shard_map/ppermute | solution.py:359
  91.8 1.1 convolution_subtract_fusion.1
  92.9 3.5 %collective-permute-start.26 = (f32[32,256]{1,0:T(8,128)S(1)}, f32[32,256]{1,0:T(8,128)S(1)}, u32[]{:S(2)}, u32[]{:S(2)}) collective-permute-start(f32[32,256]{1,0:T(8,128)S(1)} %add.156), channel_id=1, source_target_pairs={{0,192},{64,0},{128,64},{192,128},{1,193},{65,1},{129,65},{193,129... | collective-permute-start | bytes 98312 | tf_op jit(solution)/shard_map/ppermute | solution.py:359
  96.4 0.7 collective-permute-start.25
  97.1 0.7 collective-permute-start.24
  97.8 1.7 %collective-permute-start.17 = (f32[64,512]{1,0:T(8,128)S(1)}, f32[64,512]{1,0:T(8,128)S(1)}, u32[]{:S(2)}, u32[]{:S(2)}) collective-permute-start(f32[64,512]{1,0:T(8,128)S(1)} %get-tuple-element.33), channel_id=1, source_target_pairs={{0,128},{64,192},{128,0},{192,64},{1,129},{65,193},{129,1},{193,65... | collective-permute-start | bytes 393224 | tf_op jit(solution)/shard_map/ppermute | solution.py:359
  99.5 1.0 collective-permute-start.16
  100.5 1.7 %collective-permute-start.18 = (f32[64,512]{1,0:T(8,128)S(1)}, f32[64,512]{1,0:T(8,128)S(1)}, u32[]{:S(2)}, u32[]{:S(2)}) collective-permute-start(f32[64,512]{1,0:T(8,128)S(1)} %get-tuple-element.33), channel_id=1, source_target_pairs={{0,192},{64,0},{128,64},{192,128},{1,193},{65,1},{129,65},{193,129... | collective-permute-start | bytes 393224 | tf_op jit(solution)/shard_map/ppermute | solution.py:359
  102.2 0.7 broadcast_in_dim.55
  102.9 5.6 %all-to-all-start.1 = ((f32[8,32,256]{2,1,0:T(8,128)}), f32[8,32,256]{2,1,0:T(8,128)S(1)}, u32[]{:S(2)}, u32[]{:S(2)}) async-start(f32[8,32,256]{2,1,0:T(8,128)} %broadcast_in_dim.55), calls=%async_computation.1 | async-start | bytes 524288 | tf_op jit(solution)/shard_map/all_to_all | solution.py:350
  108.6 0.8 pad_maximum_fusion.cols_ref
  109.4 2.0 %collective-permute-start.19 = (f32[4,64,512]{2,1,0:T(8,128)}, f32[4,64,512]{2,1,0:T(8,128)}, u32[]{:S(2)}, u32[]{:S(2)}) collective-permute-start(f32[4,64,512]{2,1,0:T(8,128)} %pad_maximum_fusion.cols_ref), channel_id=1, source_target_pairs={{0,32},{32,0},{1,33},{33,1},{2,34},{34,2},{3,35},{35,3},{4,36},{36... | collective-permute-start | bytes 1572872 | tf_op jit(solution)/shard_map/ppermute | solution.py:359
  111.4 2.5 %fusion.y_ref = f32[2048,256]{1,0:T(8,128)S(1)} fusion(f32[256,256]{1,0:T(8,128)S(1)} %get-tuple-element.16.inv_ref, f32[2048,256]{1,0:T(8,128)} %panel_ref.3, f32[256]{0:T(256)S(1)} %bitcast.72, s32[2048]{0:T(1024)S(1)} %copy-done.6), kind=kOutput, calls=%fused_computation.1 | convolution fusion | flops 806879232 | bytes 4465664 | tf_op jit(solution)/shard_map/dot_general | solution.py:21
  114.2 1.2 collective-permute-start.14
  115.4 0.8 collective-permute-start.13
  116.2 1.6 %all-to-all-done.1 = f32[8,32,256]{2,1,0:T(8,128)S(1)} async-done(((f32[8,32,256]{2,1,0:T(8,128)}), f32[8,32,256]{2,1,0:T(8,128)S(1)}, u32[]{:S(2)}, u32[]{:S(2)}) %all-to-all-start.1) | async-done | bytes 262176 | tf_op jit(solution)/shard_map/all_to_all | solution.py:350
  118.7 2.4 %right_kernel.1.right_ref = bf16[1536,512]{1,0:T(8,128)(2,1)S(1)} custom-call(s32[3]{0:T(128)S(1)} %pad_add_fusion.place_ref, f32[4,64,512]{2,1,0:T(8,128)} %pad_maximum_fusion.cols_ref, f32[4,64,512]{2,1,0:T(8,128)} %collective-permute-done.19.other_ref, f32[256,256]{1,0:T(8,128)S(1)} %shard_map.44.block_ref, f32[256,256]{1,0:T(8,128)S(1)} %fusion.13.coupling_ref), custom_call_target="tpu_custom_call" | custom-call | flops 2000000000 | bytes 1048576 | tf_op jit(solution)/shard_map/right_kernel/pallas_call | solution.py:320
  121.2 6.4 %collective-permute-done.15.down_ref = f32[512,256]{1,0:T(8,128)} collective-permute-done((f32[512,256]{1,0:T(8,128)S(1)}, f32[512,256]{1,0:T(8,128)}, u32[]{:S(2)}, u32[]{:S(2)}) %collective-permute-start.15) | collective-permute-done | bytes 524320 | tf_op jit(solution)/shard_map/ppermute | solution.py:359
  127.6 1.5 collective-permute-done.14.over_ref
  129.0 11.9 %collective-permute-done.13.up_ref = f32[512,256]{1,0:T(8,128)} collective-permute-done((f32[512,256]{1,0:T(8,128)S(1)}, f32[512,256]{1,0:T(8,128)}, u32[]{:S(2)}, u32[]{:S(2)}) %collective-permute-start.13) | collective-permute-done | bytes 524320 | tf_op jit(solution)/shard_map/ppermute | solution.py:359
  140.9 7.4 %update_kernel.1 = f32[2048,512]{1,0:T(8,128)} custom-call(s32[3]{0:T(128)S(1)} %pad_add_fusion.place_ref, f32[2048,512]{1,0:T(8,128)S(1)} %copy-done.1, f32[2048,256]{1,0:T(8,128)S(1)} %fusion.y_ref, f32[512,256]{1,0:T(8,128)S(1)} %bitcast.59, f32[512,256]{1,0:T(8,128)} %collective-permute-done.13.up_ref, f32[512,256]{1,0:T(8,128)} %collective-permute-done.14.over_ref, ...), custom_call_target="tpu_custom_call" | custom-call | flops 2000000000 | bytes 1048576 | tf_op jit(solution)/shard_map/update_kernel/pallas_call | solution.py:331
  (62 shorter events, 5.7 us)
Async XLA Ops:
  0.7 1.6 %copy-start.2 = (f32[2048,256]{1,0:T(8,128)S(1)}, f32[2048,256]{1,0:T(8,128)}, u32[]{:S(2)}) copy-start(f32[2048,256]{1,0:T(8,128)} %panel_ref.3) | copy-start | bytes 6291460
  2.3 6.0 %copy-start.3 = (f32[2048,256]{1,0:T(8,128)S(1)}, f32[2048,256]{1,0:T(8,128)}, u32[]{:S(2)}) copy-start(f32[2048,256]{1,0:T(8,128)} %panel_ref.3) | copy-start | bytes 6291460
  5.0 10.4 %collective-permute-start = (f32[4,32,512]{2,1,0:T(8,128)S(1)}, f32[4,32,512]{2,1,0:T(8,128)S(1)}, u32[]{:S(2)}, u32[]{:S(2)}) collective-permute-start(f32[4,32,512]{2,1,0:T(8,128)S(1)} %get-tuple-element.15), channel_id=1, source_target_pairs={{0,32},{32,0},{1,33},{33,1},{2,34},{34,2},{3,35},{35,3},{4,36},{36... | collective-permute-start | bytes 786440 | tf_op jit(solution)/shard_map/ppermute | solution.py:359
  8.3 2.2 %copy-start = (f32[2048,512]{1,0:T(8,128)S(1)}, f32[2048,512]{1,0:T(8,128)}, u32[]{:S(2)}) copy-start(f32[2048,512]{1,0:T(8,128)} %trailing_ref.3) | copy-start | bytes 12582916
  15.3 9.8 %collective-permute-start.8 = (f32[4,64,512]{2,1,0:T(8,128)}, f32[4,64,512]{2,1,0:T(8,128)}, u32[]{:S(2)}, u32[]{:S(2)}) collective-permute-start(f32[4,64,512]{2,1,0:T(8,128)} %get-tuple-element.19), channel_id=1, source_target_pairs={{0,32},{32,0},{1,33},{33,1},{2,34},{34,2},{3,35},{35,3},{4,36},{36... | collective-permute-start | bytes 1572872 | tf_op jit(solution)/shard_map/ppermute | solution.py:359
  15.4 4.4 %collective-permute-start.1 = (f32[32,512]{1,0:T(8,128)S(1)}, f32[32,512]{1,0:T(8,128)S(1)}, u32[]{:S(2)}, u32[]{:S(2)}) collective-permute-start(f32[32,512]{1,0:T(8,128)S(1)} %get-tuple-element.29), channel_id=1, source_target_pairs={{0,64},{64,128},{128,192},{192,0},{1,65},{65,129},{129,193},{193,1... | collective-permute-start | bytes 196616 | tf_op jit(solution)/shard_map/ppermute | solution.py:359
  15.5 4.6 %collective-permute-start.3 = (f32[32,512]{1,0:T(8,128)S(1)}, f32[32,512]{1,0:T(8,128)S(1)}, u32[]{:S(2)}, u32[]{:S(2)}) collective-permute-start(f32[32,512]{1,0:T(8,128)S(1)} %get-tuple-element.30), channel_id=1, source_target_pairs={{0,192},{64,0},{128,64},{192,128},{1,193},{65,1},{129,65},{193,129... | collective-permute-start | bytes 196616 | tf_op jit(solution)/shard_map/ppermute | solution.py:359
  18.2 4.6 %collective-permute-start.2 = (f32[32,512]{1,0:T(8,128)S(1)}, f32[32,512]{1,0:T(8,128)S(1)}, u32[]{:S(2)}, u32[]{:S(2)}) collective-permute-start(f32[32,512]{1,0:T(8,128)S(1)} %get-tuple-element.31), channel_id=1, source_target_pairs={{0,128},{64,192},{128,0},{192,64},{1,129},{65,193},{129,1},{193,65... | collective-permute-start | bytes 196616 | tf_op jit(solution)/shard_map/ppermute | solution.py:359
  22.8 8.1 %collective-permute-start.6 = (f32[32,512]{1,0:T(8,128)S(1)}, f32[32,512]{1,0:T(8,128)S(1)}, u32[]{:S(2)}, u32[]{:S(2)}) collective-permute-start(f32[32,512]{1,0:T(8,128)S(1)} %fusion.8), channel_id=1, source_target_pairs={{0,192},{64,0},{128,64},{192,128},{1,193},{65,1},{129,65},{193,129... | collective-permute-start | bytes 196616 | tf_op jit(solution)/shard_map/ppermute | solution.py:359
  24.5 8.0 %collective-permute-start.5 = (f32[32,512]{1,0:T(8,128)S(1)}, f32[32,512]{1,0:T(8,128)S(1)}, u32[]{:S(2)}, u32[]{:S(2)}) collective-permute-start(f32[32,512]{1,0:T(8,128)S(1)} %fusion.8), channel_id=1, source_target_pairs={{0,128},{64,192},{128,0},{192,64},{1,129},{65,193},{129,1},{193,65... | collective-permute-start | bytes 196616 | tf_op jit(solution)/shard_map/ppermute | solution.py:359
  24.5 8.0 %collective-permute-start.4 = (f32[32,512]{1,0:T(8,128)S(1)}, f32[32,512]{1,0:T(8,128)S(1)}, u32[]{:S(2)}, u32[]{:S(2)}) collective-permute-start(f32[32,512]{1,0:T(8,128)S(1)} %fusion.8), channel_id=1, source_target_pairs={{0,64},{64,128},{128,192},{192,0},{1,65},{65,129},{129,193},{193,1... | collective-permute-start | bytes 196616 | tf_op jit(solution)/shard_map/ppermute | solution.py:359
  28.1 8.3 %collective-permute-start.9 = (f32[64,512]{1,0:T(8,128)S(1)}, f32[64,512]{1,0:T(8,128)S(1)}, u32[]{:S(2)}, u32[]{:S(2)}) collective-permute-start(f32[64,512]{1,0:T(8,128)S(1)} %get-tuple-element.26), channel_id=1, source_target_pairs={{0,64},{64,128},{128,192},{192,0},{1,65},{65,129},{129,193},{193,1... | collective-permute-start | bytes 393224 | tf_op jit(solution)/shard_map/ppermute | solution.py:359
  30.2 6.3 %collective-permute-start.11 = (f32[64,512]{1,0:T(8,128)S(1)}, f32[64,512]{1,0:T(8,128)S(1)}, u32[]{:S(2)}, u32[]{:S(2)}) collective-permute-start(f32[64,512]{1,0:T(8,128)S(1)} %get-tuple-element.27), channel_id=1, source_target_pairs={{0,192},{64,0},{128,64},{192,128},{1,193},{65,1},{129,65},{193,129... | collective-permute-start | bytes 393224 | tf_op jit(solution)/shard_map/ppermute | solution.py:359
  30.9 6.4 %collective-permute-start.10 = (f32[64,512]{1,0:T(8,128)S(1)}, f32[64,512]{1,0:T(8,128)S(1)}, u32[]{:S(2)}, u32[]{:S(2)}) collective-permute-start(f32[64,512]{1,0:T(8,128)S(1)} %get-tuple-element.28), channel_id=1, source_target_pairs={{0,128},{64,192},{128,0},{192,64},{1,129},{65,193},{129,1},{193,65... | collective-permute-start | bytes 393224 | tf_op jit(solution)/shard_map/ppermute | solution.py:359
  32.5 11.5 %collective-permute-start.7 = (f32[4,32,512]{2,1,0:T(8,128)S(1)}, f32[4,32,512]{2,1,0:T(8,128)S(1)}, u32[]{:S(2)}, u32[]{:S(2)}) collective-permute-start(f32[4,32,512]{2,1,0:T(8,128)S(1)} %pad_maximum_fusion.1.sums_ref), channel_id=1, source_target_pairs={{0,32},{32,0},{1,33},{33,1},{2,34},{34,2},{3,35},{35,3},{4,36},{36... | collective-permute-start | bytes 786440 | tf_op jit(solution)/shard_map/ppermute | solution.py:359
  38.2 16.3 %collective-permute-start.12 = (f32[64,768]{1,0:T(8,128)S(1)}, f32[64,768]{1,0:T(8,128)S(1)}, u32[]{:S(2)}, u32[]{:S(2)}) collective-permute-start(f32[64,768]{1,0:T(8,128)S(1)} %pad_maximum_fusion.2), channel_id=1, source_target_pairs={{0,0},{1,1},{2,2},{3,3},{4,32},{5,33},{6,34},{7,35},{8,64},{9,65},... | collective-permute-start | bytes 589832 | tf_op jit(solution)/shard_map/ppermute | solution.py:424
  54.6 0.7 copy-start.5
  56.4 20.6 %all-to-all-start = ((f32[8,64,256]{2,1,0:T(8,128)}), f32[8,64,256]{2,1,0:T(8,128)S(1)}, u32[]{:S(2)}, u32[]{:S(2)}) async-start(f32[8,64,256]{2,1,0:T(8,128)} %broadcast_in_dim.53), calls=%async_computation | async-start | bytes 1048576 | tf_op jit(solution)/shard_map/all_to_all | solution.py:350
  65.3 11.6 %copy-start.4 = (f32[512,256]{1,0:T(8,128)S(1)}, f32[512,256]{1,0:T(8,128)}, u32[]{:S(2)}) copy-start(f32[512,256]{1,0:T(8,128)} %convolution_subtract_fusion) | copy-start | bytes 1572868
  65.3 26.4 %copy-start.7 = (s32[64]{0:T(128)S(1)}, s32[64]{0:T(128)}, u32[]{:S(2)}) copy-start(s32[64]{0:T(128)} %iota_add_fusion.2) | copy-start | bytes 772
  78.0 33.4 %copy-start.6 = (s32[2048]{0:T(1024)S(1)}, s32[2048]{0:T(1024)}, u32[]{:S(2)}) copy-start(s32[2048]{0:T(1024)} %iota_add_fusion) | copy-start | bytes 24580
  78.0 4.1 %collective-permute-start.22 = (f32[32,256]{1,0:T(8,128)S(1)}, f32[32,256]{1,0:T(8,128)S(1)}, u32[]{:S(2)}, u32[]{:S(2)}) collective-permute-start(f32[32,256]{1,0:T(8,128)S(1)} %constant_dynamic-slice_fusion), channel_id=1, source_target_pairs={{0,3},{1,0},{2,1},{3,2},{4,7},{5,4},{6,5},{7,6},{8,11},{9,8},{10,9... | collective-permute-start | bytes 98312 | tf_op jit(solution)/shard_map/ppermute | solution.py:359
  80.8 4.3 %collective-permute-start.21 = (f32[32,256]{1,0:T(8,128)S(1)}, f32[32,256]{1,0:T(8,128)S(1)}, u32[]{:S(2)}, u32[]{:S(2)}) collective-permute-start(f32[32,256]{1,0:T(8,128)S(1)} %constant_dynamic-slice_fusion), channel_id=1, source_target_pairs={{0,2},{1,3},{2,0},{3,1},{4,6},{5,7},{6,4},{7,5},{8,10},{9,11},{10,... | collective-permute-start | bytes 98312 | tf_op jit(solution)/shard_map/ppermute | solution.py:359
  81.2 4.3 %collective-permute-start.20 = (f32[32,256]{1,0:T(8,128)S(1)}, f32[32,256]{1,0:T(8,128)S(1)}, u32[]{:S(2)}, u32[]{:S(2)}) collective-permute-start(f32[32,256]{1,0:T(8,128)S(1)} %constant_dynamic-slice_fusion), channel_id=1, source_target_pairs={{0,1},{1,2},{2,3},{3,0},{4,5},{5,6},{6,7},{7,4},{8,9},{9,10},{10,1... | collective-permute-start | bytes 98312 | tf_op jit(solution)/shard_map/ppermute | solution.py:359
  85.4 7.5 %collective-permute-start.23 = (f32[32,256]{1,0:T(8,128)S(1)}, f32[32,256]{1,0:T(8,128)S(1)}, u32[]{:S(2)}, u32[]{:S(2)}) collective-permute-start(f32[32,256]{1,0:T(8,128)S(1)} %add_add_fusion.1), channel_id=1, source_target_pairs={{0,32},{32,0},{1,33},{33,1},{2,34},{34,2},{3,35},{35,3},{4,36},{36... | collective-permute-start | bytes 98312 | tf_op jit(solution)/shard_map/ppermute | solution.py:359
  92.9 7.6 %collective-permute-start.26 = (f32[32,256]{1,0:T(8,128)S(1)}, f32[32,256]{1,0:T(8,128)S(1)}, u32[]{:S(2)}, u32[]{:S(2)}) collective-permute-start(f32[32,256]{1,0:T(8,128)S(1)} %add.156), channel_id=1, source_target_pairs={{0,192},{64,0},{128,64},{192,128},{1,193},{65,1},{129,65},{193,129... | collective-permute-start | bytes 98312 | tf_op jit(solution)/shard_map/ppermute | solution.py:359
  96.4 5.8 %collective-permute-start.25 = (f32[32,256]{1,0:T(8,128)S(1)}, f32[32,256]{1,0:T(8,128)S(1)}, u32[]{:S(2)}, u32[]{:S(2)}) collective-permute-start(f32[32,256]{1,0:T(8,128)S(1)} %add.156), channel_id=1, source_target_pairs={{0,128},{64,192},{128,0},{192,64},{1,129},{65,193},{129,1},{193,65... | collective-permute-start | bytes 98312 | tf_op jit(solution)/shard_map/ppermute | solution.py:359
  97.1 5.1 %collective-permute-start.24 = (f32[32,256]{1,0:T(8,128)S(1)}, f32[32,256]{1,0:T(8,128)S(1)}, u32[]{:S(2)}, u32[]{:S(2)}) collective-permute-start(f32[32,256]{1,0:T(8,128)S(1)} %add.156), channel_id=1, source_target_pairs={{0,64},{64,128},{128,192},{192,0},{1,65},{65,129},{129,193},{193,1... | collective-permute-start | bytes 98312 | tf_op jit(solution)/shard_map/ppermute | solution.py:359
  97.8 10.7 %collective-permute-start.17 = (f32[64,512]{1,0:T(8,128)S(1)}, f32[64,512]{1,0:T(8,128)S(1)}, u32[]{:S(2)}, u32[]{:S(2)}) collective-permute-start(f32[64,512]{1,0:T(8,128)S(1)} %get-tuple-element.33), channel_id=1, source_target_pairs={{0,128},{64,192},{128,0},{192,64},{1,129},{65,193},{129,1},{193,65... | collective-permute-start | bytes 393224 | tf_op jit(solution)/shard_map/ppermute | solution.py:359
  99.5 9.0 %collective-permute-start.16 = (f32[64,512]{1,0:T(8,128)S(1)}, f32[64,512]{1,0:T(8,128)S(1)}, u32[]{:S(2)}, u32[]{:S(2)}) collective-permute-start(f32[64,512]{1,0:T(8,128)S(1)} %get-tuple-element.33), channel_id=1, source_target_pairs={{0,64},{64,128},{128,192},{192,0},{1,65},{65,129},{129,193},{193,1... | collective-permute-start | bytes 393224 | tf_op jit(solution)/shard_map/ppermute | solution.py:359
  100.5 8.1 %collective-permute-start.18 = (f32[64,512]{1,0:T(8,128)S(1)}, f32[64,512]{1,0:T(8,128)S(1)}, u32[]{:S(2)}, u32[]{:S(2)}) collective-permute-start(f32[64,512]{1,0:T(8,128)S(1)} %get-tuple-element.33), channel_id=1, source_target_pairs={{0,192},{64,0},{128,64},{192,128},{1,193},{65,1},{129,65},{193,129... | collective-permute-start | bytes 393224 | tf_op jit(solution)/shard_map/ppermute | solution.py:359
  102.9 14.8 %all-to-all-start.1 = ((f32[8,32,256]{2,1,0:T(8,128)}), f32[8,32,256]{2,1,0:T(8,128)S(1)}, u32[]{:S(2)}, u32[]{:S(2)}) async-start(f32[8,32,256]{2,1,0:T(8,128)} %broadcast_in_dim.55), calls=%async_computation.1 | async-start | bytes 524288 | tf_op jit(solution)/shard_map/all_to_all | solution.py:350
  109.4 9.3 %collective-permute-start.19 = (f32[4,64,512]{2,1,0:T(8,128)}, f32[4,64,512]{2,1,0:T(8,128)}, u32[]{:S(2)}, u32[]{:S(2)}) collective-permute-start(f32[4,64,512]{2,1,0:T(8,128)} %pad_maximum_fusion.cols_ref), channel_id=1, source_target_pairs={{0,32},{32,0},{1,33},{33,1},{2,34},{34,2},{3,35},{35,3},{4,36},{36... | collective-permute-start | bytes 1572872 | tf_op jit(solution)/shard_map/ppermute | solution.py:359
  113.9 13.7 %collective-permute-start.15 = (f32[512,256]{1,0:T(8,128)S(1)}, f32[512,256]{1,0:T(8,128)}, u32[]{:S(2)}, u32[]{:S(2)}) collective-permute-start(f32[512,256]{1,0:T(8,128)S(1)} %bitcast.56), channel_id=1, source_target_pairs={{0,3},{1,0},{2,1},{3,2},{4,7},{5,4},{6,5},{7,6},{8,11},{9,8},{10,9... | collective-permute-start | bytes 1572872 | tf_op jit(solution)/shard_map/ppermute | solution.py:359
  114.2 14.9 %collective-permute-start.14 = (f32[512,256]{1,0:T(8,128)S(1)}, f32[512,256]{1,0:T(8,128)}, u32[]{:S(2)}, u32[]{:S(2)}) collective-permute-start(f32[512,256]{1,0:T(8,128)S(1)} %bitcast.57), channel_id=1, source_target_pairs={{0,2},{1,3},{2,0},{3,1},{4,6},{5,7},{6,4},{7,5},{8,10},{9,11},{10,... | collective-permute-start | bytes 1572872 | tf_op jit(solution)/shard_map/ppermute | solution.py:359
  115.4 25.5 %collective-permute-start.13 = (f32[512,256]{1,0:T(8,128)S(1)}, f32[512,256]{1,0:T(8,128)}, u32[]{:S(2)}, u32[]{:S(2)}) collective-permute-start(f32[512,256]{1,0:T(8,128)S(1)} %bitcast.58), channel_id=1, source_target_pairs={{0,1},{1,2},{2,3},{3,0},{4,5},{5,6},{6,7},{7,4},{8,9},{9,10},{10,1... | collective-permute-start | bytes 1572872 | tf_op jit(solution)/shard_map/ppermute | solution.py:359
  118.7 22.2 %copy-start.1 = (f32[2048,512]{1,0:T(8,128)S(1)}, f32[2048,512]{1,0:T(8,128)}, u32[]{:S(2)}) copy-start(f32[2048,512]{1,0:T(8,128)} %trailing_ref.3) | copy-start | bytes 12582916
where the time goes:
time: 149 us
  starting transfers between devices  58.3 us (39%)
  Pallas kernels  39.5 us (27%)
  waiting for transfers between devices  30 us (20%)
  matrix products  7.38 us (5%)
  local copies, waits for them, and re-layouts  7.15 us (5%)
  other arithmetic  5.05 us (3%)
    ppermute x26, starting transfers between devices, shift(): return lax.ppermute(x, axis, [(i, (i + by) % n) for i in range(n)])  40.3 us
    ppermute x26, waiting for transfers between devices, shift(): return lax.ppermute(x, axis, [(i, (i + by) % n) for i in range(n)])  28.5 us
    pallas_call x2, Pallas kernels, local_call(): pl.pallas_call(kernel, out_shape=[jax.ShapeDtypeStruct(s, jnp.float32) fo...  22.2 us
    all_to_all x2, starting transfers between devices, exchange(): return lax.all_to_all(x, axis, 0, 0, tiled=True)  12.2 us
    pallas_call x2, Pallas kernels, stream_call(): pl.pallas_call(kernel, out_shape=[jax.ShapeDtypeStruct(out, jnp.float32)]...  7.52 us
    pallas_call x1, Pallas kernels, update_call(): pl.pallas_call(update_kernel, name='update_kernel', out_shape=jax.ShapeDt...  7.44 us
    dot_general x8, matrix products, dot(): lax.dot_general(left, right, (dims, ((), ())), precision=precision, prefe...  7.38 us
    ppermute x1, starting transfers between devices, shards(): lax.ppermute(jnp.concatenate([pieces, to_swap], axis=1), ALL, swap)  5.73 us
  transfers between devices with their start and end apart: 29, of which 10 were waited for; matrix products, arithmetic and copies ran while one was open for 9% of the time, Pallas kernels for 20%

commit v1 on v0

--- a/solution.py
+++ b/solution.py
@@ -144,32 +144,49 @@
     share_out(core, cross, slice(width, 2 * width), kept_ref, sent_ref)
 
 
-def product_kernel(place_ref, trailing_ref, panel_ref, kept_ref, sent_ref, total, edge):
-    width = panel_ref.shape[1]
-    rows = panel_ref.shape[0] // STEPS
+def product_kernel(
+    place_ref, trailing_ref, panel_ref, kept_ref, sent_ref,
+    trailing, panel, total, edge, semaphores,
+):
+    width = panel.shape[1]
+    rows = panel.shape[0] // STEPS
     core = place_ref[1]
     first = (place_ref[0] + core == 0).astype(jnp.float32)
-    edge[...] = trailing_ref[:width].T * first
+
+    def copies(c):
+        at = pl.ds(pl.multiple_of(c * rows, rows), rows)
+        return (
+            pltpu.make_async_copy(trailing_ref.at[at], trailing.at[at], semaphores.at[0, c]),
+            pltpu.make_async_copy(panel_ref.at[at], panel.at[at], semaphores.at[1, c]),
+        )
+
+    for c in range(STEPS):
+        for copy in copies(c):
+            copy.start()
     total[...] = jnp.zeros_like(total)
 
     @pl.loop(0, STEPS)
     def _(c):
+        for copy in copies(c):
+            copy.wait()
         at = pl.ds(pl.multiple_of(c * rows, rows), rows)
-        total[...] += dot3(halves(trailing_ref[at, :].T), halves(panel_ref[at, :]), ((1,), (0,)))
-
+        total[...] += dot3(halves(trailing[at, :].T), halves(panel[at, :]), ((1,), (0,)))
+
+    edge[...] = trailing[:width].T * first
     share_out(core, total, slice(0, width), kept_ref, sent_ref)
     share_out(core, edge, slice(width, 2 * width), kept_ref, sent_ref)
 
 
-def stream_call(kernel, place, arrays, out, scratch, flops):
+def stream_call(kernel, place, arrays, out, scratch, flops, copies=()):
     vmem = pl.BlockSpec(memory_space=pltpu.VMEM)
+    inputs = pl.BlockSpec(memory_space=pl.ANY) if copies else vmem
     return pl.pallas_call(
         kernel,
         out_shape=[jax.ShapeDtypeStruct(out, jnp.float32)] * 2,
-        in_specs=[pl.BlockSpec(memory_space=pltpu.SMEM)] + [vmem] * len(arrays),
+        in_specs=[pl.BlockSpec(memory_space=pltpu.SMEM)] + [inputs] * len(arrays),
         out_specs=[vmem] * 2,
-        scratch_shapes=[pltpu.VMEM(s, jnp.float32) for s in scratch],
-        compiler_params=pltpu.CompilerParams(vmem_limit_bytes=24 * 2**20),
+        scratch_shapes=[pltpu.VMEM(s, jnp.float32) for s in scratch] + list(copies),
+        compiler_params=pltpu.CompilerParams(vmem_limit_bytes=(60 if copies else 24) * 2**20),
         cost_estimate=estimate(flops),
     )(place, *arrays)
 
@@ -208,13 +225,11 @@
     sign_ref[...] = jnp.broadcast_to(row, sign_ref.shape)
 
 
-def block_kernel(top_ref, inv_ref, sign_ref, out_ref, work, side):
-    width = top_ref.shape[0]
-    work[:, :width] = unit_eye(width) - nt(inv_ref[...], top_ref[...]) * sign_ref[0:1, :]
-    work[:, width:] = unit_eye(width)
+def sweep(work, side, first, last):
+    width = work.shape[0]
     index = lax.broadcasted_iota(jnp.int32, (width, 1), 0)
 
-    @pl.loop(0, width // NB)
+    @pl.loop(first, last)
     def _(k):
         lo = pl.multiple_of(k * NB, NB)
         cols = at_block(k, work[:, :width], NB)
@@ -225,6 +240,18 @@
         work[...] = work[...] - dot3(halves(cols), halves(rows), ((1,), (0,)))
         work[pl.ds(lo, NB), :] = rows
 
+
+def block_first(top_ref, inv_ref, sign_ref, work, side):
+    width = top_ref.shape[0]
+    work[:, :width] = unit_eye(width) - nt(inv_ref[...], top_ref[...]) * sign_ref[0:1, :]
+    work[:, width:] = unit_eye(width)
+    sweep(work, side, 0, width // NB // 2)
+
+
+def block_second(state_ref, out_ref, work, side):
+    width = out_ref.shape[0]
+    work[...] = state_ref[...]
+    sweep(work, side, width // NB // 2, width // NB)
     out_ref[...] = work[:, width:]
 
 
@@ -415,8 +442,9 @@
         place,
         [trailing, panel],
         (x_n, piece, 2 * width),
-        [(local_cols, width)] * 2,
+        [trailing.shape, panel.shape] + [(local_cols, width)] * 2,
         2 * 10**9,
+        [pltpu.SemaphoreType.DMA((2, STEPS))],
     )
     pieces = scatter_sum(pair_sum(kept, sent), "x")
     mine = lax.dynamic_slice_in_dim(panel, y * local_cols, local_cols, 0)
@@ -434,12 +462,19 @@
         in_specs=[smem, vmem, vmem],
         cost_estimate=estimate(3 * 10**9),
     )
+    (state,) = local_call(
+        block_first,
+        [(width, 2 * width)],
+        [((width, NB), jnp.float32)],
+        top, inv, sign,
+        cost_estimate=estimate(2 * 10**9),
+    )
     (block,) = local_call(
-        block_kernel,
+        block_second,
         [(width, width)],
         [((width, 2 * width), jnp.float32), ((width, NB), jnp.float32)],
-        top, inv, sign,
-        cost_estimate=estimate(4 * 10**9),
+        state,
+        cost_estimate=estimate(2 * 10**9),
     )
     sign = sign[0:1]
 

time: 149 us -> 146 us (0.980)
  local copies, waits for them, and re-layouts: 7.15 us -> 4.09 us
  other arithmetic: 5.05 us -> 2.23 us
  Pallas kernels: 39.5 us -> 41.3 us
    unnamed x16 -> x8, local copies, waits for them, and re-layouts: 4.48 us -> 1.61 us
    pallas_call x2, Pallas kernels: 7.52 us -> 9.21 us  [stream_call(): pl.pallas_call(kernel, out_shape=[jax.ShapeDtypeStruct(out, jnp.float32)]...]
    pallas_call x2 -> x3, Pallas kernels: 22.2 us -> 22.2 us  [local_call(): pl.pallas_call(kernel, out_shape=[jax.ShapeDtypeStruct(s, jnp.float32) fo...]
  transfers between devices with their start and end apart: 29 -> 29, of which waited for: 10 -> 11; matrix products, arithmetic and copies ran while one was open for 9% -> 6% of each run, Pallas kernels for 20% -> 21%
where the time goes in v1:
time: 146 us; the launch traced here: 145 us
  starting transfers between devices  59.6 us (41%)
  Pallas kernels  41.3 us (28%)
  waiting for transfers between devices  30 us (21%)
  matrix products  6.79 us (5%)
  local copies, waits for them, and re-layouts  4.09 us (3%)
  other arithmetic  2.23 us (2%)
    ppermute x26, starting transfers between devices, shift(): return lax.ppermute(x, axis, [(i, (i + by) % n) for i in range(n)])  40.6 us
    ppermute x26, waiting for transfers between devices, shift(): return lax.ppermute(x, axis, [(i, (i + by) % n) for i in range(n)])  28.5 us
    pallas_call x3, Pallas kernels, local_call(): pl.pallas_call(kernel, out_shape=[jax.ShapeDtypeStruct(s, jnp.float32) fo...  22.2 us
    all_to_all x2, starting transfers between devices, exchange(): return lax.all_to_all(x, axis, 0, 0, tiled=True)  13.4 us
    pallas_call x2, Pallas kernels, stream_call(): pl.pallas_call(kernel, out_shape=[jax.ShapeDtypeStruct(out, jnp.float32)]...  9.21 us
    pallas_call x1, Pallas kernels, update_call(): pl.pallas_call(update_kernel, name='update_kernel', out_shape=jax.ShapeDt...  7.44 us
    dot_general x8, matrix products, dot(): lax.dot_general(left, right, (dims, ((), ())), precision=precision, prefe...  6.79 us
    ppermute x1, starting transfers between devices, shards(): lax.ppermute(jnp.concatenate([pieces, to_swap], axis=1), ALL, swap)  5.54 us
  transfers between devices with their start and end apart: 29, of which 11 were waited for; matrix products, arithmetic and copies ran while one was open for 6% of the time, Pallas kernels for 21%

profile of v1, /device:TPU:1, one launch (start us, length us, event | category | flops | bytes accessed | tf_op | source)
XLA Modules:
  0.0 145.1 jit_solution(7971622601312707909)
XLA Ops:
  0.7 1.6 %copy-done.1 = f32[2048,256]{1,0:T(8,128)S(1)} copy-done((f32[2048,256]{1,0:T(8,128)S(1)}, f32[2048,256]{1,0:T(8,128)}, u32[]{:S(2)}) %copy-start.1) | copy-done | bytes 2097176
  2.3 2.7 %shard_map.41 = (f32[4,32,512]{2,1,0:T(8,128)S(1)}, f32[4,32,512]{2,1,0:T(8,128)S(1)}) custom-call(s32[3]{0:T(128)S(1)} %pad_add_fusion.place_ref, f32[2048,256]{1,0:T(8,128)S(1)} %copy-done.1), custom_call_target="tpu_custom_call" | custom-call | flops 1000000000 | bytes 1048576 | tf_op jit(solution)/shard_map/pallas_call | solution.py:183
  5.0 3.3 %collective-permute-start = (f32[4,32,512]{2,1,0:T(8,128)S(1)}, f32[4,32,512]{2,1,0:T(8,128)S(1)}, u32[]{:S(2)}, u32[]{:S(2)}) collective-permute-start(f32[4,32,512]{2,1,0:T(8,128)S(1)} %get-tuple-element.15), channel_id=1, source_target_pairs={{0,32},{32,0},{1,33},{33,1},{2,34},{34,2},{3,35},{35,3},{4,36},{36... | collective-permute-start | bytes 786440 | tf_op jit(solution)/shard_map/ppermute | solution.py:386
  8.3 6.6 %shard_map.43 = (f32[4,64,512]{2,1,0:T(8,128)}, f32[4,64,512]{2,1,0:T(8,128)}) custom-call(s32[3]{0:T(128)} %copy-done.2, f32[2048,512]{1,0:T(8,128)} %trailing_ref.3, f32[2048,256]{1,0:T(8,128)} %panel_ref.3), custom_call_target="tpu_custom_call" | custom-call | flops 2000000000 | bytes 1048576 | tf_op jit(solution)/shard_map/pallas_call | solution.py:183
  15.1 2.7 %collective-permute-start.3 = (f32[32,512]{1,0:T(8,128)S(1)}, f32[32,512]{1,0:T(8,128)S(1)}, u32[]{:S(2)}, u32[]{:S(2)}) collective-permute-start(f32[32,512]{1,0:T(8,128)S(1)} %get-tuple-element.30), channel_id=1, source_target_pairs={{0,192},{64,0},{128,64},{192,128},{1,193},{65,1},{129,65},{193,129... | collective-permute-start | bytes 196616 | tf_op jit(solution)/shard_map/ppermute | solution.py:386
  17.8 1.6 %collective-permute-done.1 = f32[32,512]{1,0:T(8,128)S(1)} collective-permute-done((f32[32,512]{1,0:T(8,128)S(1)}, f32[32,512]{1,0:T(8,128)S(1)}, u32[]{:S(2)}, u32[]{:S(2)}) %collective-permute-start.1) | collective-permute-done | bytes 65568 | tf_op jit(solution)/shard_map/ppermute | solution.py:386
  19.8 2.6 %collective-permute-done.2 = f32[32,512]{1,0:T(8,128)S(1)} collective-permute-done((f32[32,512]{1,0:T(8,128)S(1)}, f32[32,512]{1,0:T(8,128)S(1)}, u32[]{:S(2)}, u32[]{:S(2)}) %collective-permute-start.2) | collective-permute-done | bytes 65568 | tf_op jit(solution)/shard_map/ppermute | solution.py:386
  22.5 1.7 %collective-permute-start.6 = (f32[32,512]{1,0:T(8,128)S(1)}, f32[32,512]{1,0:T(8,128)S(1)}, u32[]{:S(2)}, u32[]{:S(2)}) collective-permute-start(f32[32,512]{1,0:T(8,128)S(1)} %fusion.8), channel_id=1, source_target_pairs={{0,192},{64,0},{128,64},{192,128},{1,193},{65,1},{129,65},{193,129... | collective-permute-start | bytes 196616 | tf_op jit(solution)/shard_map/ppermute | solution.py:386
  24.2 0.7 collective-permute-start.4
  24.9 1.1 add.144
  26.0 2.0 %collective-permute-start.9 = (f32[64,512]{1,0:T(8,128)S(1)}, f32[64,512]{1,0:T(8,128)S(1)}, u32[]{:S(2)}, u32[]{:S(2)}) collective-permute-start(f32[64,512]{1,0:T(8,128)S(1)} %get-tuple-element.26), channel_id=1, source_target_pairs={{0,64},{64,128},{128,192},{192,0},{1,65},{65,129},{129,193},{193,1... | collective-permute-start | bytes 393224 | tf_op jit(solution)/shard_map/ppermute | solution.py:386
  28.1 0.7 collective-permute-start.11
  28.8 1.5 %collective-permute-start.10 = (f32[64,512]{1,0:T(8,128)S(1)}, f32[64,512]{1,0:T(8,128)S(1)}, u32[]{:S(2)}, u32[]{:S(2)}) collective-permute-start(f32[64,512]{1,0:T(8,128)S(1)} %get-tuple-element.28), channel_id=1, source_target_pairs={{0,128},{64,192},{128,0},{192,64},{1,129},{65,193},{129,1},{193,65... | collective-permute-start | bytes 393224 | tf_op jit(solution)/shard_map/ppermute | solution.py:386
  30.3 0.8 constant_dynamic-slice_fusion.1
  31.2 3.9 %collective-permute-start.7 = (f32[4,32,512]{2,1,0:T(8,128)S(1)}, f32[4,32,512]{2,1,0:T(8,128)S(1)}, u32[]{:S(2)}, u32[]{:S(2)}) collective-permute-start(f32[4,32,512]{2,1,0:T(8,128)S(1)} %pad_maximum_fusion.1.sums_ref), channel_id=1, source_target_pairs={{0,32},{32,0},{1,33},{33,1},{2,34},{34,2},{3,35},{35,3},{4,36},{36... | collective-permute-start | bytes 786440 | tf_op jit(solution)/shard_map/ppermute | solution.py:386
  35.3 5.5 %collective-permute-start.12 = (f32[64,768]{1,0:T(8,128)S(1)}, f32[64,768]{1,0:T(8,128)S(1)}, u32[]{:S(2)}, u32[]{:S(2)}) collective-permute-start(f32[64,768]{1,0:T(8,128)S(1)} %pad_maximum_fusion.2), channel_id=1, source_target_pairs={{0,0},{1,1},{2,2},{3,3},{4,32},{5,33},{6,34},{7,35},{8,64},{9,65},... | collective-permute-start | bytes 589832 | tf_op jit(solution)/shard_map/ppermute | solution.py:452
  40.9 10.6 %shard_map.42 = (f32[256,256]{1,0:T(8,128)}, f32[256,256]{1,0:T(8,128)S(1)}, f32[8,256]{1,0:T(8,128)S(1)}, f32[256,256]{1,0:T(8,128)S(1)}) custom-call(s32[3]{0:T(128)S(1)} %copy-done.3, f32[4,32,512]{2,1,0:T(8,128)S(1)} %pad_maximum_fusion.1.sums_ref, f32[4,32,512]{2,1,0:T(8,128)S(1)} %collective-permute-done.7.other_ref), custom_call_target="tpu_custom_call" | custom-call | flops 3000000000 | bytes 1048576 | tf_op jit(solution)/shard_map/pallas_call | solution.py:326
  51.7 0.8 broadcast_in_dim.53
  52.6 7.5 %all-to-all-start = ((f32[8,64,256]{2,1,0:T(8,128)}), f32[8,64,256]{2,1,0:T(8,128)S(1)}, u32[]{:S(2)}, u32[]{:S(2)}) async-start(f32[8,64,256]{2,1,0:T(8,128)} %broadcast_in_dim.53), calls=%async_computation | async-start | bytes 1048576 | tf_op jit(solution)/shard_map/all_to_all | solution.py:377
  60.1 6.0 %shard_map.44.state_ref = f32[256,512]{1,0:T(8,128)S(1)} custom-call(f32[256,256]{1,0:T(8,128)S(1)} %get-tuple-element.20.top_ref, f32[256,256]{1,0:T(8,128)S(1)} %get-tuple-element.16.inv_ref, f32[8,256]{1,0:T(8,128)S(1)} %get-tuple-element.17.sign_ref), custom_call_target="tpu_custom_call" | custom-call | flops 2000000000 | bytes 1048576 | tf_op jit(solution)/shard_map/pallas_call | solution.py:326
  66.1 5.6 %shard_map.45.block_ref = f32[256,256]{1,0:T(8,128)S(1)} custom-call(f32[256,512]{1,0:T(8,128)S(1)} %shard_map.44.state_ref), custom_call_target="tpu_custom_call" | custom-call | flops 2000000000 | bytes 1048576 | tf_op jit(solution)/shard_map/pallas_call | solution.py:326
  71.8 1.5 %convolution_subtract_fusion = f32[512,256]{1,0:T(8,128)S(1)} fusion(f32[256,256]{1,0:T(8,128)S(1)} %get-tuple-element.16.inv_ref, f32[2048,256]{1,0:T(8,128)} %panel_ref.3, s32[]{:T(128)S(6)} %select_n.80, f32[256]{0:T(256)S(1)} %bitcast.69, s32[512]{0:T(512)S(1)} %iota_add_fusion.1), kind=kOutput, calls=%fused_computation.3 | convolution fusion | flops 201719808 | bytes 1313796 | tf_op jit(solution)/shard_map/dot_general | solution.py:21
  73.3 1.0 fusion.11
  74.3 2.8 %collective-permute-start.22 = (f32[32,256]{1,0:T(8,128)S(1)}, f32[32,256]{1,0:T(8,128)S(1)}, u32[]{:S(2)}, u32[]{:S(2)}) collective-permute-start(f32[32,256]{1,0:T(8,128)S(1)} %constant_dynamic-slice_fusion), channel_id=1, source_target_pairs={{0,3},{1,0},{2,1},{3,2},{4,7},{5,4},{6,5},{7,6},{8,11},{9,8},{10,9... | collective-permute-start | bytes 98312 | tf_op jit(solution)/shard_map/ppermute | solution.py:386
  77.5 0.7 collective-permute-start.20
  78.5 3.0 %collective-permute-done.21 = f32[32,256]{1,0:T(8,128)S(1)} collective-permute-done((f32[32,256]{1,0:T(8,128)S(1)}, f32[32,256]{1,0:T(8,128)S(1)}, u32[]{:S(2)}, u32[]{:S(2)}) %collective-permute-start.21) | collective-permute-done | bytes 32800 | tf_op jit(solution)/shard_map/ppermute | solution.py:386
  81.7 6.8 %collective-permute-start.23 = (f32[32,256]{1,0:T(8,128)S(1)}, f32[32,256]{1,0:T(8,128)S(1)}, u32[]{:S(2)}, u32[]{:S(2)}) collective-permute-start(f32[32,256]{1,0:T(8,128)S(1)} %add_add_fusion.1), channel_id=1, source_target_pairs={{0,32},{32,0},{1,33},{33,1},{2,34},{34,2},{3,35},{35,3},{4,36},{36... | collective-permute-start | bytes 98312 | tf_op jit(solution)/shard_map/ppermute | solution.py:386
  88.9 0.6 collective-permute-done.23
  89.5 2.1 %collective-permute-start.26 = (f32[32,256]{1,0:T(8,128)S(1)}, f32[32,256]{1,0:T(8,128)S(1)}, u32[]{:S(2)}, u32[]{:S(2)}) collective-permute-start(f32[32,256]{1,0:T(8,128)S(1)} %add.156), channel_id=1, source_target_pairs={{0,192},{64,0},{128,64},{192,128},{1,193},{65,1},{129,65},{193,129... | collective-permute-start | bytes 98312 | tf_op jit(solution)/shard_map/ppermute | solution.py:386
  91.5 1.8 %collective-permute-start.25 = (f32[32,256]{1,0:T(8,128)S(1)}, f32[32,256]{1,0:T(8,128)S(1)}, u32[]{:S(2)}, u32[]{:S(2)}) collective-permute-start(f32[32,256]{1,0:T(8,128)S(1)} %add.156), channel_id=1, source_target_pairs={{0,128},{64,192},{128,0},{192,64},{1,129},{65,193},{129,1},{193,65... | collective-permute-start | bytes 98312 | tf_op jit(solution)/shard_map/ppermute | solution.py:386
  93.4 2.0 %collective-permute-start.17 = (f32[64,512]{1,0:T(8,128)S(1)}, f32[64,512]{1,0:T(8,128)S(1)}, u32[]{:S(2)}, u32[]{:S(2)}) collective-permute-start(f32[64,512]{1,0:T(8,128)S(1)} %get-tuple-element.33), channel_id=1, source_target_pairs={{0,128},{64,192},{128,0},{192,64},{1,129},{65,193},{129,1},{193,65... | collective-permute-start | bytes 393224 | tf_op jit(solution)/shard_map/ppermute | solution.py:386
  95.4 1.4 collective-permute-start.16
  96.7 1.3 collective-permute-start.18
  98.1 0.7 broadcast_in_dim.55
  98.8 5.9 %all-to-all-start.1 = ((f32[8,32,256]{2,1,0:T(8,128)}), f32[8,32,256]{2,1,0:T(8,128)S(1)}, u32[]{:S(2)}, u32[]{:S(2)}) async-start(f32[8,32,256]{2,1,0:T(8,128)} %broadcast_in_dim.55), calls=%async_computation.1 | async-start | bytes 524288 | tf_op jit(solution)/shard_map/all_to_all | solution.py:377
  104.7 0.8 pad_maximum_fusion.cols_ref
  105.6 2.3 %collective-permute-start.19 = (f32[4,64,512]{2,1,0:T(8,128)}, f32[4,64,512]{2,1,0:T(8,128)}, u32[]{:S(2)}, u32[]{:S(2)}) collective-permute-start(f32[4,64,512]{2,1,0:T(8,128)} %pad_maximum_fusion.cols_ref), channel_id=1, source_target_pairs={{0,32},{32,0},{1,33},{33,1},{2,34},{34,2},{3,35},{35,3},{4,36},{36... | collective-permute-start | bytes 1572872 | tf_op jit(solution)/shard_map/ppermute | solution.py:386
  107.9 2.5 %fusion.y_ref = f32[2048,256]{1,0:T(8,128)S(1)} fusion(f32[256,256]{1,0:T(8,128)S(1)} %get-tuple-element.16.inv_ref, f32[2048,256]{1,0:T(8,128)} %panel_ref.3, f32[256]{0:T(256)S(1)} %bitcast.72, s32[2048]{0:T(1024)S(1)} %iota_add_fusion), kind=kOutput, calls=%fused_computation.1 | convolution fusion | flops 806879232 | bytes 4465664 | tf_op jit(solution)/shard_map/dot_general | solution.py:21
  110.8 1.2 collective-permute-start.14
  112.0 0.8 collective-permute-start.13
  112.7 1.5 %all-to-all-done.1 = f32[8,32,256]{2,1,0:T(8,128)S(1)} async-done(((f32[8,32,256]{2,1,0:T(8,128)}), f32[8,32,256]{2,1,0:T(8,128)S(1)}, u32[]{:S(2)}, u32[]{:S(2)}) %all-to-all-start.1) | async-done | bytes 262176 | tf_op jit(solution)/shard_map/all_to_all | solution.py:377
  114.2 0.4 fusion.12
  114.6 0.6 fusion.13.coupling_ref
  115.2 2.4 %right_kernel.1.right_ref = bf16[1536,512]{1,0:T(8,128)(2,1)S(1)} custom-call(s32[3]{0:T(128)S(1)} %copy-done.3, f32[4,64,512]{2,1,0:T(8,128)} %pad_maximum_fusion.cols_ref, f32[4,64,512]{2,1,0:T(8,128)} %collective-permute-done.19.other_ref, f32[256,256]{1,0:T(8,128)S(1)} %shard_map.45.block_ref, f32[256,256]{1,0:T(8,128)S(1)} %fusion.13.coupling_ref), custom_call_target="tpu_custom_call" | custom-call | flops 2000000000 | bytes 1048576 | tf_op jit(solution)/shard_map/right_kernel/pallas_call | solution.py:347
  117.6 6.4 %collective-permute-done.15.down_ref = f32[512,256]{1,0:T(8,128)} collective-permute-done((f32[512,256]{1,0:T(8,128)S(1)}, f32[512,256]{1,0:T(8,128)}, u32[]{:S(2)}, u32[]{:S(2)}) %collective-permute-start.15) | collective-permute-done | bytes 524320 | tf_op jit(solution)/shard_map/ppermute | solution.py:386
  124.1 1.5 %collective-permute-done.14.over_ref = f32[512,256]{1,0:T(8,128)} collective-permute-done((f32[512,256]{1,0:T(8,128)S(1)}, f32[512,256]{1,0:T(8,128)}, u32[]{:S(2)}, u32[]{:S(2)}) %collective-permute-start.14) | collective-permute-done | bytes 524320 | tf_op jit(solution)/shard_map/ppermute | solution.py:386
  125.6 11.9 %collective-permute-done.13.up_ref = f32[512,256]{1,0:T(8,128)} collective-permute-done((f32[512,256]{1,0:T(8,128)S(1)}, f32[512,256]{1,0:T(8,128)}, u32[]{:S(2)}, u32[]{:S(2)}) %collective-permute-start.13) | collective-permute-done | bytes 524320 | tf_op jit(solution)/shard_map/ppermute | solution.py:386
  137.5 7.4 %update_kernel.1 = f32[2048,512]{1,0:T(8,128)} custom-call(s32[3]{0:T(128)S(1)} %copy-done.3, f32[2048,512]{1,0:T(8,128)S(1)} %copy-done, f32[2048,256]{1,0:T(8,128)S(1)} %fusion.y_ref, f32[512,256]{1,0:T(8,128)S(1)} %bitcast.59, f32[512,256]{1,0:T(8,128)} %collective-permute-done.13.up_ref, f32[512,256]{1,0:T(8,128)} %collective-permute-done.14.over_ref, ...), custom_call_target="tpu_custom_call" | custom-call | flops 2000000000 | bytes 1048576 | tf_op jit(solution)/shard_map/update_kernel/pallas_call | solution.py:358
  (55 shorter events, 2.9 us)
Async XLA Ops:
  0.7 1.6 %copy-start.1 = (f32[2048,256]{1,0:T(8,128)S(1)}, f32[2048,256]{1,0:T(8,128)}, u32[]{:S(2)}) copy-start(f32[2048,256]{1,0:T(8,128)} %panel_ref.3) | copy-start | bytes 6291460
  2.3 6.0 %copy-start.2 = (s32[3]{0:T(128)}, s32[3]{0:T(128)S(1)}, u32[]{:S(2)}) copy-start(s32[3]{0:T(128)S(1)} %pad_add_fusion.place_ref) | copy-start | bytes 40
  5.0 10.0 %collective-permute-start = (f32[4,32,512]{2,1,0:T(8,128)S(1)}, f32[4,32,512]{2,1,0:T(8,128)S(1)}, u32[]{:S(2)}, u32[]{:S(2)}) collective-permute-start(f32[4,32,512]{2,1,0:T(8,128)S(1)} %get-tuple-element.15), channel_id=1, source_target_pairs={{0,32},{32,0},{1,33},{33,1},{2,34},{34,2},{3,35},{35,3},{4,36},{36... | collective-permute-start | bytes 786440 | tf_op jit(solution)/shard_map/ppermute | solution.py:386
  14.8 10.0 %collective-permute-start.8 = (f32[4,64,512]{2,1,0:T(8,128)}, f32[4,64,512]{2,1,0:T(8,128)S(1)}, u32[]{:S(2)}, u32[]{:S(2)}) collective-permute-start(f32[4,64,512]{2,1,0:T(8,128)} %get-tuple-element.19), channel_id=1, source_target_pairs={{0,32},{32,0},{1,33},{33,1},{2,34},{34,2},{3,35},{35,3},{4,36},{36... | collective-permute-start | bytes 1572872 | tf_op jit(solution)/shard_map/ppermute | solution.py:386
  15.1 4.4 %collective-permute-start.1 = (f32[32,512]{1,0:T(8,128)S(1)}, f32[32,512]{1,0:T(8,128)S(1)}, u32[]{:S(2)}, u32[]{:S(2)}) collective-permute-start(f32[32,512]{1,0:T(8,128)S(1)} %get-tuple-element.29), channel_id=1, source_target_pairs={{0,64},{64,128},{128,192},{192,0},{1,65},{65,129},{129,193},{193,1... | collective-permute-start | bytes 196616 | tf_op jit(solution)/shard_map/ppermute | solution.py:386
  15.1 4.7 %collective-permute-start.3 = (f32[32,512]{1,0:T(8,128)S(1)}, f32[32,512]{1,0:T(8,128)S(1)}, u32[]{:S(2)}, u32[]{:S(2)}) collective-permute-start(f32[32,512]{1,0:T(8,128)S(1)} %get-tuple-element.30), channel_id=1, source_target_pairs={{0,192},{64,0},{128,64},{192,128},{1,193},{65,1},{129,65},{193,129... | collective-permute-start | bytes 196616 | tf_op jit(solution)/shard_map/ppermute | solution.py:386
  17.8 4.6 %collective-permute-start.2 = (f32[32,512]{1,0:T(8,128)S(1)}, f32[32,512]{1,0:T(8,128)S(1)}, u32[]{:S(2)}, u32[]{:S(2)}) collective-permute-start(f32[32,512]{1,0:T(8,128)S(1)} %get-tuple-element.31), channel_id=1, source_target_pairs={{0,128},{64,192},{128,0},{192,64},{1,129},{65,193},{129,1},{193,65... | collective-permute-start | bytes 196616 | tf_op jit(solution)/shard_map/ppermute | solution.py:386
  22.5 18.4 %copy-start.3 = (s32[3]{0:T(128)S(1)}, s32[3]{0:T(128)}, u32[]{:S(2)}) copy-start(s32[3]{0:T(128)} %copy-done.2) | copy-start | bytes 40
  22.5 6.3 %collective-permute-start.6 = (f32[32,512]{1,0:T(8,128)S(1)}, f32[32,512]{1,0:T(8,128)S(1)}, u32[]{:S(2)}, u32[]{:S(2)}) collective-permute-start(f32[32,512]{1,0:T(8,128)S(1)} %fusion.8), channel_id=1, source_target_pairs={{0,192},{64,0},{128,64},{192,128},{1,193},{65,1},{129,65},{193,129... | collective-permute-start | bytes 196616 | tf_op jit(solution)/shard_map/ppermute | solution.py:386
  24.2 7.0 %collective-permute-start.5 = (f32[32,512]{1,0:T(8,128)S(1)}, f32[32,512]{1,0:T(8,128)S(1)}, u32[]{:S(2)}, u32[]{:S(2)}) collective-permute-start(f32[32,512]{1,0:T(8,128)S(1)} %fusion.8), channel_id=1, source_target_pairs={{0,128},{64,192},{128,0},{192,64},{1,129},{65,193},{129,1},{193,65... | collective-permute-start | bytes 196616 | tf_op jit(solution)/shard_map/ppermute | solution.py:386
  24.2 7.0 %collective-permute-start.4 = (f32[32,512]{1,0:T(8,128)S(1)}, f32[32,512]{1,0:T(8,128)S(1)}, u32[]{:S(2)}, u32[]{:S(2)}) collective-permute-start(f32[32,512]{1,0:T(8,128)S(1)} %fusion.8), channel_id=1, source_target_pairs={{0,64},{64,128},{128,192},{192,0},{1,65},{65,129},{129,193},{193,1... | collective-permute-start | bytes 196616 | tf_op jit(solution)/shard_map/ppermute | solution.py:386
  26.0 9.1 %collective-permute-start.9 = (f32[64,512]{1,0:T(8,128)S(1)}, f32[64,512]{1,0:T(8,128)S(1)}, u32[]{:S(2)}, u32[]{:S(2)}) collective-permute-start(f32[64,512]{1,0:T(8,128)S(1)} %get-tuple-element.26), channel_id=1, source_target_pairs={{0,64},{64,128},{128,192},{192,0},{1,65},{65,129},{129,193},{193,1... | collective-permute-start | bytes 393224 | tf_op jit(solution)/shard_map/ppermute | solution.py:386
  28.1 7.0 %collective-permute-start.11 = (f32[64,512]{1,0:T(8,128)S(1)}, f32[64,512]{1,0:T(8,128)S(1)}, u32[]{:S(2)}, u32[]{:S(2)}) collective-permute-start(f32[64,512]{1,0:T(8,128)S(1)} %get-tuple-element.27), channel_id=1, source_target_pairs={{0,192},{64,0},{128,64},{192,128},{1,193},{65,1},{129,65},{193,129... | collective-permute-start | bytes 393224 | tf_op jit(solution)/shard_map/ppermute | solution.py:386
  28.8 6.5 %collective-permute-start.10 = (f32[64,512]{1,0:T(8,128)S(1)}, f32[64,512]{1,0:T(8,128)S(1)}, u32[]{:S(2)}, u32[]{:S(2)}) collective-permute-start(f32[64,512]{1,0:T(8,128)S(1)} %get-tuple-element.28), channel_id=1, source_target_pairs={{0,128},{64,192},{128,0},{192,64},{1,129},{65,193},{129,1},{193,65... | collective-permute-start | bytes 393224 | tf_op jit(solution)/shard_map/ppermute | solution.py:386
  31.2 9.7 %collective-permute-start.7 = (f32[4,32,512]{2,1,0:T(8,128)S(1)}, f32[4,32,512]{2,1,0:T(8,128)S(1)}, u32[]{:S(2)}, u32[]{:S(2)}) collective-permute-start(f32[4,32,512]{2,1,0:T(8,128)S(1)} %pad_maximum_fusion.1.sums_ref), channel_id=1, source_target_pairs={{0,32},{32,0},{1,33},{33,1},{2,34},{34,2},{3,35},{35,3},{4,36},{36... | collective-permute-start | bytes 786440 | tf_op jit(solution)/shard_map/ppermute | solution.py:386
  35.3 16.1 %collective-permute-start.12 = (f32[64,768]{1,0:T(8,128)S(1)}, f32[64,768]{1,0:T(8,128)S(1)}, u32[]{:S(2)}, u32[]{:S(2)}) collective-permute-start(f32[64,768]{1,0:T(8,128)S(1)} %pad_maximum_fusion.2), channel_id=1, source_target_pairs={{0,0},{1,1},{2,2},{3,3},{4,32},{5,33},{6,34},{7,35},{8,64},{9,65},... | collective-permute-start | bytes 589832 | tf_op jit(solution)/shard_map/ppermute | solution.py:452
  52.6 20.7 %all-to-all-start = ((f32[8,64,256]{2,1,0:T(8,128)}), f32[8,64,256]{2,1,0:T(8,128)S(1)}, u32[]{:S(2)}, u32[]{:S(2)}) async-start(f32[8,64,256]{2,1,0:T(8,128)} %broadcast_in_dim.53), calls=%async_computation | async-start | bytes 1048576 | tf_op jit(solution)/shard_map/all_to_all | solution.py:377
  74.3 4.1 %collective-permute-start.22 = (f32[32,256]{1,0:T(8,128)S(1)}, f32[32,256]{1,0:T(8,128)S(1)}, u32[]{:S(2)}, u32[]{:S(2)}) collective-permute-start(f32[32,256]{1,0:T(8,128)S(1)} %constant_dynamic-slice_fusion), channel_id=1, source_target_pairs={{0,3},{1,0},{2,1},{3,2},{4,7},{5,4},{6,5},{7,6},{8,11},{9,8},{10,9... | collective-permute-start | bytes 98312 | tf_op jit(solution)/shard_map/ppermute | solution.py:386
  77.1 4.3 %collective-permute-start.21 = (f32[32,256]{1,0:T(8,128)S(1)}, f32[32,256]{1,0:T(8,128)S(1)}, u32[]{:S(2)}, u32[]{:S(2)}) collective-permute-start(f32[32,256]{1,0:T(8,128)S(1)} %constant_dynamic-slice_fusion), channel_id=1, source_target_pairs={{0,2},{1,3},{2,0},{3,1},{4,6},{5,7},{6,4},{7,5},{8,10},{9,11},{10,... | collective-permute-start | bytes 98312 | tf_op jit(solution)/shard_map/ppermute | solution.py:386
  77.5 4.3 %collective-permute-start.20 = (f32[32,256]{1,0:T(8,128)S(1)}, f32[32,256]{1,0:T(8,128)S(1)}, u32[]{:S(2)}, u32[]{:S(2)}) collective-permute-start(f32[32,256]{1,0:T(8,128)S(1)} %constant_dynamic-slice_fusion), channel_id=1, source_target_pairs={{0,1},{1,2},{2,3},{3,0},{4,5},{5,6},{6,7},{7,4},{8,9},{9,10},{10,1... | collective-permute-start | bytes 98312 | tf_op jit(solution)/shard_map/ppermute | solution.py:386
  81.7 7.7 %collective-permute-start.23 = (f32[32,256]{1,0:T(8,128)S(1)}, f32[32,256]{1,0:T(8,128)S(1)}, u32[]{:S(2)}, u32[]{:S(2)}) collective-permute-start(f32[32,256]{1,0:T(8,128)S(1)} %add_add_fusion.1), channel_id=1, source_target_pairs={{0,32},{32,0},{1,33},{33,1},{2,34},{34,2},{3,35},{35,3},{4,36},{36... | collective-permute-start | bytes 98312 | tf_op jit(solution)/shard_map/ppermute | solution.py:386
  89.5 7.3 %collective-permute-start.26 = (f32[32,256]{1,0:T(8,128)S(1)}, f32[32,256]{1,0:T(8,128)S(1)}, u32[]{:S(2)}, u32[]{:S(2)}) collective-permute-start(f32[32,256]{1,0:T(8,128)S(1)} %add.156), channel_id=1, source_target_pairs={{0,192},{64,0},{128,64},{192,128},{1,193},{65,1},{129,65},{193,129... | collective-permute-start | bytes 98312 | tf_op jit(solution)/shard_map/ppermute | solution.py:386
  91.5 6.5 %collective-permute-start.25 = (f32[32,256]{1,0:T(8,128)S(1)}, f32[32,256]{1,0:T(8,128)S(1)}, u32[]{:S(2)}, u32[]{:S(2)}) collective-permute-start(f32[32,256]{1,0:T(8,128)S(1)} %add.156), channel_id=1, source_target_pairs={{0,128},{64,192},{128,0},{192,64},{1,129},{65,193},{129,1},{193,65... | collective-permute-start | bytes 98312 | tf_op jit(solution)/shard_map/ppermute | solution.py:386
  93.4 4.7 %collective-permute-start.24 = (f32[32,256]{1,0:T(8,128)S(1)}, f32[32,256]{1,0:T(8,128)S(1)}, u32[]{:S(2)}, u32[]{:S(2)}) collective-permute-start(f32[32,256]{1,0:T(8,128)S(1)} %add.156), channel_id=1, source_target_pairs={{0,64},{64,128},{128,192},{192,0},{1,65},{65,129},{129,193},{193,1... | collective-permute-start | bytes 98312 | tf_op jit(solution)/shard_map/ppermute | solution.py:386
  93.4 11.3 %collective-permute-start.17 = (f32[64,512]{1,0:T(8,128)S(1)}, f32[64,512]{1,0:T(8,128)S(1)}, u32[]{:S(2)}, u32[]{:S(2)}) collective-permute-start(f32[64,512]{1,0:T(8,128)S(1)} %get-tuple-element.33), channel_id=1, source_target_pairs={{0,128},{64,192},{128,0},{192,64},{1,129},{65,193},{129,1},{193,65... | collective-permute-start | bytes 393224 | tf_op jit(solution)/shard_map/ppermute | solution.py:386
  95.4 9.4 %collective-permute-start.16 = (f32[64,512]{1,0:T(8,128)S(1)}, f32[64,512]{1,0:T(8,128)S(1)}, u32[]{:S(2)}, u32[]{:S(2)}) collective-permute-start(f32[64,512]{1,0:T(8,128)S(1)} %get-tuple-element.33), channel_id=1, source_target_pairs={{0,64},{64,128},{128,192},{192,0},{1,65},{65,129},{129,193},{193,1... | collective-permute-start | bytes 393224 | tf_op jit(solution)/shard_map/ppermute | solution.py:386
  96.7 8.0 %collective-permute-start.18 = (f32[64,512]{1,0:T(8,128)S(1)}, f32[64,512]{1,0:T(8,128)S(1)}, u32[]{:S(2)}, u32[]{:S(2)}) collective-permute-start(f32[64,512]{1,0:T(8,128)S(1)} %get-tuple-element.33), channel_id=1, source_target_pairs={{0,192},{64,0},{128,64},{192,128},{1,193},{65,1},{129,65},{193,129... | collective-permute-start | bytes 393224 | tf_op jit(solution)/shard_map/ppermute | solution.py:386
  98.8 15.4 %all-to-all-start.1 = ((f32[8,32,256]{2,1,0:T(8,128)}), f32[8,32,256]{2,1,0:T(8,128)S(1)}, u32[]{:S(2)}, u32[]{:S(2)}) async-start(f32[8,32,256]{2,1,0:T(8,128)} %broadcast_in_dim.55), calls=%async_computation.1 | async-start | bytes 524288 | tf_op jit(solution)/shard_map/all_to_all | solution.py:377
  105.6 9.6 %collective-permute-start.19 = (f32[4,64,512]{2,1,0:T(8,128)}, f32[4,64,512]{2,1,0:T(8,128)}, u32[]{:S(2)}, u32[]{:S(2)}) collective-permute-start(f32[4,64,512]{2,1,0:T(8,128)} %pad_maximum_fusion.cols_ref), channel_id=1, source_target_pairs={{0,32},{32,0},{1,33},{33,1},{2,34},{34,2},{3,35},{35,3},{4,36},{36... | collective-permute-start | bytes 1572872 | tf_op jit(solution)/shard_map/ppermute | solution.py:386
  110.4 13.7 %collective-permute-start.15 = (f32[512,256]{1,0:T(8,128)S(1)}, f32[512,256]{1,0:T(8,128)}, u32[]{:S(2)}, u32[]{:S(2)}) collective-permute-start(f32[512,256]{1,0:T(8,128)S(1)} %bitcast.56), channel_id=1, source_target_pairs={{0,3},{1,0},{2,1},{3,2},{4,7},{5,4},{6,5},{7,6},{8,11},{9,8},{10,9... | collective-permute-start | bytes 1572872 | tf_op jit(solution)/shard_map/ppermute | solution.py:386
  110.8 14.8 %collective-permute-start.14 = (f32[512,256]{1,0:T(8,128)S(1)}, f32[512,256]{1,0:T(8,128)}, u32[]{:S(2)}, u32[]{:S(2)}) collective-permute-start(f32[512,256]{1,0:T(8,128)S(1)} %bitcast.57), channel_id=1, source_target_pairs={{0,2},{1,3},{2,0},{3,1},{4,6},{5,7},{6,4},{7,5},{8,10},{9,11},{10,... | collective-permute-start | bytes 1572872 | tf_op jit(solution)/shard_map/ppermute | solution.py:386
  112.0 25.5 %collective-permute-start.13 = (f32[512,256]{1,0:T(8,128)S(1)}, f32[512,256]{1,0:T(8,128)}, u32[]{:S(2)}, u32[]{:S(2)}) collective-permute-start(f32[512,256]{1,0:T(8,128)S(1)} %bitcast.58), channel_id=1, source_target_pairs={{0,1},{1,2},{2,3},{3,0},{4,5},{5,6},{6,7},{7,4},{8,9},{9,10},{10,1... | collective-permute-start | bytes 1572872 | tf_op jit(solution)/shard_map/ppermute | solution.py:386
  115.2 22.3 %copy-start = (f32[2048,512]{1,0:T(8,128)S(1)}, f32[2048,512]{1,0:T(8,128)}, u32[]{:S(2)}) copy-start(f32[2048,512]{1,0:T(8,128)} %trailing_ref.3) | copy-start | bytes 12582916

commit v2 on v1

--- a/solution.py
+++ b/solution.py
@@ -279,7 +279,7 @@
 
 def update_kernel(
     place_ref, trailing_ref, y_ref, own_ref, up_ref, over_ref, down_ref, right_ref,
-    out_ref, tile, result, left, semaphores, done,
+    out_ref, result, left, done,
 ):
     count, width = own_ref.shape
     sources = (own_ref, up_ref, over_ref, down_ref)
@@ -288,16 +288,8 @@
         to = lax.rem(place_ref[2] + len(sources) - step, len(sources))
         return pl.ds(pl.multiple_of(to * count, count), count)
 
-    def loading(step):
-        return pltpu.make_async_copy(
-            trailing_ref.at[rows_of(step)], tile.at[step], semaphores.at[step]
-        )
-
     def storing(step):
         return pltpu.make_async_copy(result.at[step], out_ref.at[rows_of(step)], done.at[step])
-
-    for step in range(len(sources)):
-        loading(step).start()
 
     @pl.loop(0, len(sources))
     def _(step):
@@ -314,8 +306,8 @@
         left[:, :width] = high
         left[:, 2 * width : 3 * width] = high
         left[:, 4 * width : 5 * width] = low
-        loading(step).wait()
-        result[step] = tile[step] - one(left[...], right_ref[...], ((1,), (0,)))
+        tile = trailing_ref[rows_of(step), :]
+        result[step] = tile - one(left[...], right_ref[...], ((1,), (0,)))
         storing(step).start()
 
     for step in range(len(sources)):
@@ -359,13 +351,11 @@
         update_kernel,
         name="update_kernel",
         out_shape=jax.ShapeDtypeStruct(trailing.shape, jnp.float32),
-        in_specs=[smem, hbm] + [vmem] * len(args),
+        in_specs=[smem, vmem] + [vmem] * len(args),
         out_specs=hbm,
         scratch_shapes=[
             pltpu.VMEM(tiles, jnp.float32),
-            pltpu.VMEM(tiles, jnp.float32),
             pltpu.VMEM((count, 6 * width), jnp.bfloat16),
-            pltpu.SemaphoreType.DMA((y_n,)),
             pltpu.SemaphoreType.DMA((y_n,)),
         ],
         compiler_params=pltpu.CompilerParams(vmem_limit_bytes=30 * 2**20),

time: 146 us -> 145 us (level)
  transfers between devices with their start and end apart: 29 -> 29, of which waited for: 11 -> 11; matrix products, arithmetic and copies ran while one was open for 6% -> 6% of each run, Pallas kernels for 21% -> 22%
where the time goes in v2:
time: 145 us; the launch traced here: 144 us
  starting transfers between devices  59.6 us (41%)
  Pallas kernels  40.5 us (28%)
  waiting for transfers between devices  30 us (21%)
  matrix products  6.79 us (5%)
  local copies, waits for them, and re-layouts  4.09 us (3%)
  other arithmetic  2.23 us (2%)
    ppermute x26, starting transfers between devices, shift(): return lax.ppermute(x, axis, [(i, (i + by) % n) for i in range(n)])  40.6 us
    ppermute x26, waiting for transfers between devices, shift(): return lax.ppermute(x, axis, [(i, (i + by) % n) for i in range(n)])  28.5 us
    pallas_call x3, Pallas kernels, local_call(): pl.pallas_call(kernel, out_shape=[jax.ShapeDtypeStruct(s, jnp.float32) fo...  22.2 us
    all_to_all x2, starting transfers between devices, exchange(): return lax.all_to_all(x, axis, 0, 0, tiled=True)  13.4 us
    pallas_call x2, Pallas kernels, stream_call(): pl.pallas_call(kernel, out_shape=[jax.ShapeDtypeStruct(out, jnp.float32)]...  9.21 us
    dot_general x8, matrix products, dot(): lax.dot_general(left, right, (dims, ((), ())), precision=precision, prefe...  6.79 us
    pallas_call x1, Pallas kernels, update_call(): pl.pallas_call(update_kernel, name='update_kernel', out_shape=jax.ShapeDt...  6.69 us
    ppermute x1, starting transfers between devices, shards(): lax.ppermute(jnp.concatenate([pieces, to_swap], axis=1), ALL, swap)  5.54 us
  transfers between devices with their start and end apart: 29, of which 11 were waited for; matrix products, arithmetic and copies ran while one was open for 6% of the time, Pallas kernels for 22%

profile of v2, /device:TPU:1, one launch (start us, length us, event | category | flops | bytes accessed | tf_op | source)
XLA Modules:
  0.0 144.4 jit_solution(4681470908330250470)
XLA Ops:
  0.7 1.6 %copy-done.1 = f32[2048,256]{1,0:T(8,128)S(1)} copy-done((f32[2048,256]{1,0:T(8,128)S(1)}, f32[2048,256]{1,0:T(8,128)}, u32[]{:S(2)}) %copy-start.1) | copy-done | bytes 2097176
  2.3 2.7 %shard_map.41 = (f32[4,32,512]{2,1,0:T(8,128)S(1)}, f32[4,32,512]{2,1,0:T(8,128)S(1)}) custom-call(s32[3]{0:T(128)S(1)} %pad_add_fusion.place_ref, f32[2048,256]{1,0:T(8,128)S(1)} %copy-done.1), custom_call_target="tpu_custom_call" | custom-call | flops 1000000000 | bytes 1048576 | tf_op jit(solution)/shard_map/pallas_call | solution.py:183
  5.0 3.3 %collective-permute-start = (f32[4,32,512]{2,1,0:T(8,128)S(1)}, f32[4,32,512]{2,1,0:T(8,128)S(1)}, u32[]{:S(2)}, u32[]{:S(2)}) collective-permute-start(f32[4,32,512]{2,1,0:T(8,128)S(1)} %get-tuple-element.15), channel_id=1, source_target_pairs={{0,32},{32,0},{1,33},{33,1},{2,34},{34,2},{3,35},{35,3},{4,36},{36... | collective-permute-start | bytes 786440 | tf_op jit(solution)/shard_map/ppermute | solution.py:376
  8.3 6.6 %shard_map.43 = (f32[4,64,512]{2,1,0:T(8,128)}, f32[4,64,512]{2,1,0:T(8,128)}) custom-call(s32[3]{0:T(128)} %copy-done.2, f32[2048,512]{1,0:T(8,128)} %trailing_ref.3, f32[2048,256]{1,0:T(8,128)} %panel_ref.3), custom_call_target="tpu_custom_call" | custom-call | flops 2000000000 | bytes 1048576 | tf_op jit(solution)/shard_map/pallas_call | solution.py:183
  15.1 2.7 %collective-permute-start.3 = (f32[32,512]{1,0:T(8,128)S(1)}, f32[32,512]{1,0:T(8,128)S(1)}, u32[]{:S(2)}, u32[]{:S(2)}) collective-permute-start(f32[32,512]{1,0:T(8,128)S(1)} %get-tuple-element.30), channel_id=1, source_target_pairs={{0,192},{64,0},{128,64},{192,128},{1,193},{65,1},{129,65},{193,129... | collective-permute-start | bytes 196616 | tf_op jit(solution)/shard_map/ppermute | solution.py:376
  17.8 1.6 %collective-permute-done.1 = f32[32,512]{1,0:T(8,128)S(1)} collective-permute-done((f32[32,512]{1,0:T(8,128)S(1)}, f32[32,512]{1,0:T(8,128)S(1)}, u32[]{:S(2)}, u32[]{:S(2)}) %collective-permute-start.1) | collective-permute-done | bytes 65568 | tf_op jit(solution)/shard_map/ppermute | solution.py:376
  19.8 2.6 %collective-permute-done.2 = f32[32,512]{1,0:T(8,128)S(1)} collective-permute-done((f32[32,512]{1,0:T(8,128)S(1)}, f32[32,512]{1,0:T(8,128)S(1)}, u32[]{:S(2)}, u32[]{:S(2)}) %collective-permute-start.2) | collective-permute-done | bytes 65568 | tf_op jit(solution)/shard_map/ppermute | solution.py:376
  22.5 1.7 %collective-permute-start.6 = (f32[32,512]{1,0:T(8,128)S(1)}, f32[32,512]{1,0:T(8,128)S(1)}, u32[]{:S(2)}, u32[]{:S(2)}) collective-permute-start(f32[32,512]{1,0:T(8,128)S(1)} %fusion.8), channel_id=1, source_target_pairs={{0,192},{64,0},{128,64},{192,128},{1,193},{65,1},{129,65},{193,129... | collective-permute-start | bytes 196616 | tf_op jit(solution)/shard_map/ppermute | solution.py:376
  24.2 0.7 collective-permute-start.4
  24.9 1.1 add.144
  26.0 2.0 %collective-permute-start.9 = (f32[64,512]{1,0:T(8,128)S(1)}, f32[64,512]{1,0:T(8,128)S(1)}, u32[]{:S(2)}, u32[]{:S(2)}) collective-permute-start(f32[64,512]{1,0:T(8,128)S(1)} %get-tuple-element.26), channel_id=1, source_target_pairs={{0,64},{64,128},{128,192},{192,0},{1,65},{65,129},{129,193},{193,1... | collective-permute-start | bytes 393224 | tf_op jit(solution)/shard_map/ppermute | solution.py:376
  28.1 0.7 collective-permute-start.11
  28.8 1.5 %collective-permute-start.10 = (f32[64,512]{1,0:T(8,128)S(1)}, f32[64,512]{1,0:T(8,128)S(1)}, u32[]{:S(2)}, u32[]{:S(2)}) collective-permute-start(f32[64,512]{1,0:T(8,128)S(1)} %get-tuple-element.28), channel_id=1, source_target_pairs={{0,128},{64,192},{128,0},{192,64},{1,129},{65,193},{129,1},{193,65... | collective-permute-start | bytes 393224 | tf_op jit(solution)/shard_map/ppermute | solution.py:376
  30.3 0.8 constant_dynamic-slice_fusion.1
  31.2 3.9 %collective-permute-start.7 = (f32[4,32,512]{2,1,0:T(8,128)S(1)}, f32[4,32,512]{2,1,0:T(8,128)S(1)}, u32[]{:S(2)}, u32[]{:S(2)}) collective-permute-start(f32[4,32,512]{2,1,0:T(8,128)S(1)} %pad_maximum_fusion.1.sums_ref), channel_id=1, source_target_pairs={{0,32},{32,0},{1,33},{33,1},{2,34},{34,2},{3,35},{35,3},{4,36},{36... | collective-permute-start | bytes 786440 | tf_op jit(solution)/shard_map/ppermute | solution.py:376
  35.3 5.5 %collective-permute-start.12 = (f32[64,768]{1,0:T(8,128)S(1)}, f32[64,768]{1,0:T(8,128)S(1)}, u32[]{:S(2)}, u32[]{:S(2)}) collective-permute-start(f32[64,768]{1,0:T(8,128)S(1)} %pad_maximum_fusion.2), channel_id=1, source_target_pairs={{0,0},{1,1},{2,2},{3,3},{4,32},{5,33},{6,34},{7,35},{8,64},{9,65},... | collective-permute-start | bytes 589832 | tf_op jit(solution)/shard_map/ppermute | solution.py:442
  40.9 10.6 %shard_map.42 = (f32[256,256]{1,0:T(8,128)}, f32[256,256]{1,0:T(8,128)S(1)}, f32[8,256]{1,0:T(8,128)S(1)}, f32[256,256]{1,0:T(8,128)S(1)}) custom-call(s32[3]{0:T(128)S(1)} %copy-done.3, f32[4,32,512]{2,1,0:T(8,128)S(1)} %pad_maximum_fusion.1.sums_ref, f32[4,32,512]{2,1,0:T(8,128)S(1)} %collective-permute-done.7.other_ref), custom_call_target="tpu_custom_call" | custom-call | flops 3000000000 | bytes 1048576 | tf_op jit(solution)/shard_map/pallas_call | solution.py:318
  51.7 0.8 broadcast_in_dim.53
  52.6 7.5 %all-to-all-start = ((f32[8,64,256]{2,1,0:T(8,128)}), f32[8,64,256]{2,1,0:T(8,128)S(1)}, u32[]{:S(2)}, u32[]{:S(2)}) async-start(f32[8,64,256]{2,1,0:T(8,128)} %broadcast_in_dim.53), calls=%async_computation | async-start | bytes 1048576 | tf_op jit(solution)/shard_map/all_to_all | solution.py:367
  60.1 6.0 %shard_map.44.state_ref = f32[256,512]{1,0:T(8,128)S(1)} custom-call(f32[256,256]{1,0:T(8,128)S(1)} %get-tuple-element.20.top_ref, f32[256,256]{1,0:T(8,128)S(1)} %get-tuple-element.16.inv_ref, f32[8,256]{1,0:T(8,128)S(1)} %get-tuple-element.17.sign_ref), custom_call_target="tpu_custom_call" | custom-call | flops 2000000000 | bytes 1048576 | tf_op jit(solution)/shard_map/pallas_call | solution.py:318
  66.1 5.6 %shard_map.45.block_ref = f32[256,256]{1,0:T(8,128)S(1)} custom-call(f32[256,512]{1,0:T(8,128)S(1)} %shard_map.44.state_ref), custom_call_target="tpu_custom_call" | custom-call | flops 2000000000 | bytes 1048576 | tf_op jit(solution)/shard_map/pallas_call | solution.py:318
  71.8 1.5 %convolution_subtract_fusion = f32[512,256]{1,0:T(8,128)S(1)} fusion(f32[256,256]{1,0:T(8,128)S(1)} %get-tuple-element.16.inv_ref, f32[2048,256]{1,0:T(8,128)} %panel_ref.3, s32[]{:T(128)S(6)} %select_n.80, f32[256]{0:T(256)S(1)} %bitcast.69, s32[512]{0:T(512)S(1)} %iota_add_fusion.1), kind=kOutput, calls=%fused_computation.3 | convolution fusion | flops 201719808 | bytes 1313796 | tf_op jit(solution)/shard_map/dot_general | solution.py:21
  73.3 1.0 fusion.11
  74.3 2.8 %collective-permute-start.22 = (f32[32,256]{1,0:T(8,128)S(1)}, f32[32,256]{1,0:T(8,128)S(1)}, u32[]{:S(2)}, u32[]{:S(2)}) collective-permute-start(f32[32,256]{1,0:T(8,128)S(1)} %constant_dynamic-slice_fusion), channel_id=1, source_target_pairs={{0,3},{1,0},{2,1},{3,2},{4,7},{5,4},{6,5},{7,6},{8,11},{9,8},{10,9... | collective-permute-start | bytes 98312 | tf_op jit(solution)/shard_map/ppermute | solution.py:376
  77.5 0.7 collective-permute-start.20
  78.5 3.0 %collective-permute-done.21 = f32[32,256]{1,0:T(8,128)S(1)} collective-permute-done((f32[32,256]{1,0:T(8,128)S(1)}, f32[32,256]{1,0:T(8,128)S(1)}, u32[]{:S(2)}, u32[]{:S(2)}) %collective-permute-start.21) | collective-permute-done | bytes 32800 | tf_op jit(solution)/shard_map/ppermute | solution.py:376
  81.7 6.8 %collective-permute-start.23 = (f32[32,256]{1,0:T(8,128)S(1)}, f32[32,256]{1,0:T(8,128)S(1)}, u32[]{:S(2)}, u32[]{:S(2)}) collective-permute-start(f32[32,256]{1,0:T(8,128)S(1)} %add_add_fusion.1), channel_id=1, source_target_pairs={{0,32},{32,0},{1,33},{33,1},{2,34},{34,2},{3,35},{35,3},{4,36},{36... | collective-permute-start | bytes 98312 | tf_op jit(solution)/shard_map/ppermute | solution.py:376
  88.9 0.6 collective-permute-done.23
  89.5 2.1 %collective-permute-start.26 = (f32[32,256]{1,0:T(8,128)S(1)}, f32[32,256]{1,0:T(8,128)S(1)}, u32[]{:S(2)}, u32[]{:S(2)}) collective-permute-start(f32[32,256]{1,0:T(8,128)S(1)} %add.156), channel_id=1, source_target_pairs={{0,192},{64,0},{128,64},{192,128},{1,193},{65,1},{129,65},{193,129... | collective-permute-start | bytes 98312 | tf_op jit(solution)/shard_map/ppermute | solution.py:376
  91.5 1.8 %collective-permute-start.25 = (f32[32,256]{1,0:T(8,128)S(1)}, f32[32,256]{1,0:T(8,128)S(1)}, u32[]{:S(2)}, u32[]{:S(2)}) collective-permute-start(f32[32,256]{1,0:T(8,128)S(1)} %add.156), channel_id=1, source_target_pairs={{0,128},{64,192},{128,0},{192,64},{1,129},{65,193},{129,1},{193,65... | collective-permute-start | bytes 98312 | tf_op jit(solution)/shard_map/ppermute | solution.py:376
  93.4 2.0 %collective-permute-start.17 = (f32[64,512]{1,0:T(8,128)S(1)}, f32[64,512]{1,0:T(8,128)S(1)}, u32[]{:S(2)}, u32[]{:S(2)}) collective-permute-start(f32[64,512]{1,0:T(8,128)S(1)} %get-tuple-element.33), channel_id=1, source_target_pairs={{0,128},{64,192},{128,0},{192,64},{1,129},{65,193},{129,1},{193,65... | collective-permute-start | bytes 393224 | tf_op jit(solution)/shard_map/ppermute | solution.py:376
  95.4 1.4 collective-permute-start.16
  96.7 1.3 collective-permute-start.18
  98.1 0.7 broadcast_in_dim.55
  98.8 5.9 %all-to-all-start.1 = ((f32[8,32,256]{2,1,0:T(8,128)}), f32[8,32,256]{2,1,0:T(8,128)S(1)}, u32[]{:S(2)}, u32[]{:S(2)}) async-start(f32[8,32,256]{2,1,0:T(8,128)} %broadcast_in_dim.55), calls=%async_computation.1 | async-start | bytes 524288 | tf_op jit(solution)/shard_map/all_to_all | solution.py:367
  104.7 0.8 pad_maximum_fusion.cols_ref
  105.6 2.3 %collective-permute-start.19 = (f32[4,64,512]{2,1,0:T(8,128)}, f32[4,64,512]{2,1,0:T(8,128)}, u32[]{:S(2)}, u32[]{:S(2)}) collective-permute-start(f32[4,64,512]{2,1,0:T(8,128)} %pad_maximum_fusion.cols_ref), channel_id=1, source_target_pairs={{0,32},{32,0},{1,33},{33,1},{2,34},{34,2},{3,35},{35,3},{4,36},{36... | collective-permute-start | bytes 1572872 | tf_op jit(solution)/shard_map/ppermute | solution.py:376
  107.9 2.5 %fusion.y_ref = f32[2048,256]{1,0:T(8,128)S(1)} fusion(f32[256,256]{1,0:T(8,128)S(1)} %get-tuple-element.16.inv_ref, f32[2048,256]{1,0:T(8,128)} %panel_ref.3, f32[256]{0:T(256)S(1)} %bitcast.72, s32[2048]{0:T(1024)S(1)} %iota_add_fusion), kind=kOutput, calls=%fused_computation.1 | convolution fusion | flops 806879232 | bytes 4465664 | tf_op jit(solution)/shard_map/dot_general | solution.py:21
  110.8 1.2 collective-permute-start.14
  112.0 0.8 collective-permute-start.13
  112.7 1.5 %all-to-all-done.1 = f32[8,32,256]{2,1,0:T(8,128)S(1)} async-done(((f32[8,32,256]{2,1,0:T(8,128)}), f32[8,32,256]{2,1,0:T(8,128)S(1)}, u32[]{:S(2)}, u32[]{:S(2)}) %all-to-all-start.1) | async-done | bytes 262176 | tf_op jit(solution)/shard_map/all_to_all | solution.py:367
  114.2 0.4 fusion.12
  114.6 0.6 fusion.13.coupling_ref
  115.2 2.4 %right_kernel.1.right_ref = bf16[1536,512]{1,0:T(8,128)(2,1)S(1)} custom-call(s32[3]{0:T(128)S(1)} %copy-done.3, f32[4,64,512]{2,1,0:T(8,128)} %pad_maximum_fusion.cols_ref, f32[4,64,512]{2,1,0:T(8,128)} %collective-permute-done.19.other_ref, f32[256,256]{1,0:T(8,128)S(1)} %shard_map.45.block_ref, f32[256,256]{1,0:T(8,128)S(1)} %fusion.13.coupling_ref), custom_call_target="tpu_custom_call" | custom-call | flops 2000000000 | bytes 1048576 | tf_op jit(solution)/shard_map/right_kernel/pallas_call | solution.py:339
  117.6 6.4 %collective-permute-done.15.down_ref = f32[512,256]{1,0:T(8,128)} collective-permute-done((f32[512,256]{1,0:T(8,128)S(1)}, f32[512,256]{1,0:T(8,128)}, u32[]{:S(2)}, u32[]{:S(2)}) %collective-permute-start.15) | collective-permute-done | bytes 524320 | tf_op jit(solution)/shard_map/ppermute | solution.py:376
  124.1 1.5 %collective-permute-done.14.over_ref = f32[512,256]{1,0:T(8,128)} collective-permute-done((f32[512,256]{1,0:T(8,128)S(1)}, f32[512,256]{1,0:T(8,128)}, u32[]{:S(2)}, u32[]{:S(2)}) %collective-permute-start.14) | collective-permute-done | bytes 524320 | tf_op jit(solution)/shard_map/ppermute | solution.py:376
  125.6 11.9 %collective-permute-done.13.up_ref = f32[512,256]{1,0:T(8,128)} collective-permute-done((f32[512,256]{1,0:T(8,128)S(1)}, f32[512,256]{1,0:T(8,128)}, u32[]{:S(2)}, u32[]{:S(2)}) %collective-permute-start.13) | collective-permute-done | bytes 524320 | tf_op jit(solution)/shard_map/ppermute | solution.py:376
  137.5 6.7 %update_kernel.1 = f32[2048,512]{1,0:T(8,128)} custom-call(s32[3]{0:T(128)S(1)} %copy-done.3, f32[2048,512]{1,0:T(8,128)S(1)} %copy-done, f32[2048,256]{1,0:T(8,128)S(1)} %fusion.y_ref, f32[512,256]{1,0:T(8,128)S(1)} %bitcast.59, f32[512,256]{1,0:T(8,128)} %collective-permute-done.13.up_ref, f32[512,256]{1,0:T(8,128)} %collective-permute-done.14.over_ref, ...), custom_call_target="tpu_custom_call" | custom-call | flops 2000000000 | bytes 1048576 | tf_op jit(solution)/shard_map/update_kernel/pallas_call | solution.py:350
  (55 shorter events, 2.9 us)
Async XLA Ops:
  0.7 1.6 %copy-start.1 = (f32[2048,256]{1,0:T(8,128)S(1)}, f32[2048,256]{1,0:T(8,128)}, u32[]{:S(2)}) copy-start(f32[2048,256]{1,0:T(8,128)} %panel_ref.3) | copy-start | bytes 6291460
  2.3 6.0 %copy-start.2 = (s32[3]{0:T(128)}, s32[3]{0:T(128)S(1)}, u32[]{:S(2)}) copy-start(s32[3]{0:T(128)S(1)} %pad_add_fusion.place_ref) | copy-start | bytes 40
  5.0 10.0 %collective-permute-start = (f32[4,32,512]{2,1,0:T(8,128)S(1)}, f32[4,32,512]{2,1,0:T(8,128)S(1)}, u32[]{:S(2)}, u32[]{:S(2)}) collective-permute-start(f32[4,32,512]{2,1,0:T(8,128)S(1)} %get-tuple-element.15), channel_id=1, source_target_pairs={{0,32},{32,0},{1,33},{33,1},{2,34},{34,2},{3,35},{35,3},{4,36},{36... | collective-permute-start | bytes 786440 | tf_op jit(solution)/shard_map/ppermute | solution.py:376
  14.8 10.0 %collective-permute-start.8 = (f32[4,64,512]{2,1,0:T(8,128)}, f32[4,64,512]{2,1,0:T(8,128)S(1)}, u32[]{:S(2)}, u32[]{:S(2)}) collective-permute-start(f32[4,64,512]{2,1,0:T(8,128)} %get-tuple-element.19), channel_id=1, source_target_pairs={{0,32},{32,0},{1,33},{33,1},{2,34},{34,2},{3,35},{35,3},{4,36},{36... | collective-permute-start | bytes 1572872 | tf_op jit(solution)/shard_map/ppermute | solution.py:376
  15.1 4.4 %collective-permute-start.1 = (f32[32,512]{1,0:T(8,128)S(1)}, f32[32,512]{1,0:T(8,128)S(1)}, u32[]{:S(2)}, u32[]{:S(2)}) collective-permute-start(f32[32,512]{1,0:T(8,128)S(1)} %get-tuple-element.29), channel_id=1, source_target_pairs={{0,64},{64,128},{128,192},{192,0},{1,65},{65,129},{129,193},{193,1... | collective-permute-start | bytes 196616 | tf_op jit(solution)/shard_map/ppermute | solution.py:376
  15.1 4.7 %collective-permute-start.3 = (f32[32,512]{1,0:T(8,128)S(1)}, f32[32,512]{1,0:T(8,128)S(1)}, u32[]{:S(2)}, u32[]{:S(2)}) collective-permute-start(f32[32,512]{1,0:T(8,128)S(1)} %get-tuple-element.30), channel_id=1, source_target_pairs={{0,192},{64,0},{128,64},{192,128},{1,193},{65,1},{129,65},{193,129... | collective-permute-start | bytes 196616 | tf_op jit(solution)/shard_map/ppermute | solution.py:376
  17.8 4.6 %collective-permute-start.2 = (f32[32,512]{1,0:T(8,128)S(1)}, f32[32,512]{1,0:T(8,128)S(1)}, u32[]{:S(2)}, u32[]{:S(2)}) collective-permute-start(f32[32,512]{1,0:T(8,128)S(1)} %get-tuple-element.31), channel_id=1, source_target_pairs={{0,128},{64,192},{128,0},{192,64},{1,129},{65,193},{129,1},{193,65... | collective-permute-start | bytes 196616 | tf_op jit(solution)/shard_map/ppermute | solution.py:376
  22.5 18.4 %copy-start.3 = (s32[3]{0:T(128)S(1)}, s32[3]{0:T(128)}, u32[]{:S(2)}) copy-start(s32[3]{0:T(128)} %copy-done.2) | copy-start | bytes 40
  22.5 6.3 %collective-permute-start.6 = (f32[32,512]{1,0:T(8,128)S(1)}, f32[32,512]{1,0:T(8,128)S(1)}, u32[]{:S(2)}, u32[]{:S(2)}) collective-permute-start(f32[32,512]{1,0:T(8,128)S(1)} %fusion.8), channel_id=1, source_target_pairs={{0,192},{64,0},{128,64},{192,128},{1,193},{65,1},{129,65},{193,129... | collective-permute-start | bytes 196616 | tf_op jit(solution)/shard_map/ppermute | solution.py:376
  24.2 7.0 %collective-permute-start.5 = (f32[32,512]{1,0:T(8,128)S(1)}, f32[32,512]{1,0:T(8,128)S(1)}, u32[]{:S(2)}, u32[]{:S(2)}) collective-permute-start(f32[32,512]{1,0:T(8,128)S(1)} %fusion.8), channel_id=1, source_target_pairs={{0,128},{64,192},{128,0},{192,64},{1,129},{65,193},{129,1},{193,65... | collective-permute-start | bytes 196616 | tf_op jit(solution)/shard_map/ppermute | solution.py:376
  24.2 7.0 %collective-permute-start.4 = (f32[32,512]{1,0:T(8,128)S(1)}, f32[32,512]{1,0:T(8,128)S(1)}, u32[]{:S(2)}, u32[]{:S(2)}) collective-permute-start(f32[32,512]{1,0:T(8,128)S(1)} %fusion.8), channel_id=1, source_target_pairs={{0,64},{64,128},{128,192},{192,0},{1,65},{65,129},{129,193},{193,1... | collective-permute-start | bytes 196616 | tf_op jit(solution)/shard_map/ppermute | solution.py:376
  26.0 9.1 %collective-permute-start.9 = (f32[64,512]{1,0:T(8,128)S(1)}, f32[64,512]{1,0:T(8,128)S(1)}, u32[]{:S(2)}, u32[]{:S(2)}) collective-permute-start(f32[64,512]{1,0:T(8,128)S(1)} %get-tuple-element.26), channel_id=1, source_target_pairs={{0,64},{64,128},{128,192},{192,0},{1,65},{65,129},{129,193},{193,1... | collective-permute-start | bytes 393224 | tf_op jit(solution)/shard_map/ppermute | solution.py:376
  28.1 7.0 %collective-permute-start.11 = (f32[64,512]{1,0:T(8,128)S(1)}, f32[64,512]{1,0:T(8,128)S(1)}, u32[]{:S(2)}, u32[]{:S(2)}) collective-permute-start(f32[64,512]{1,0:T(8,128)S(1)} %get-tuple-element.27), channel_id=1, source_target_pairs={{0,192},{64,0},{128,64},{192,128},{1,193},{65,1},{129,65},{193,129... | collective-permute-start | bytes 393224 | tf_op jit(solution)/shard_map/ppermute | solution.py:376
  28.8 6.5 %collective-permute-start.10 = (f32[64,512]{1,0:T(8,128)S(1)}, f32[64,512]{1,0:T(8,128)S(1)}, u32[]{:S(2)}, u32[]{:S(2)}) collective-permute-start(f32[64,512]{1,0:T(8,128)S(1)} %get-tuple-element.28), channel_id=1, source_target_pairs={{0,128},{64,192},{128,0},{192,64},{1,129},{65,193},{129,1},{193,65... | collective-permute-start | bytes 393224 | tf_op jit(solution)/shard_map/ppermute | solution.py:376
  31.2 9.7 %collective-permute-start.7 = (f32[4,32,512]{2,1,0:T(8,128)S(1)}, f32[4,32,512]{2,1,0:T(8,128)S(1)}, u32[]{:S(2)}, u32[]{:S(2)}) collective-permute-start(f32[4,32,512]{2,1,0:T(8,128)S(1)} %pad_maximum_fusion.1.sums_ref), channel_id=1, source_target_pairs={{0,32},{32,0},{1,33},{33,1},{2,34},{34,2},{3,35},{35,3},{4,36},{36... | collective-permute-start | bytes 786440 | tf_op jit(solution)/shard_map/ppermute | solution.py:376
  35.3 16.1 %collective-permute-start.12 = (f32[64,768]{1,0:T(8,128)S(1)}, f32[64,768]{1,0:T(8,128)S(1)}, u32[]{:S(2)}, u32[]{:S(2)}) collective-permute-start(f32[64,768]{1,0:T(8,128)S(1)} %pad_maximum_fusion.2), channel_id=1, source_target_pairs={{0,0},{1,1},{2,2},{3,3},{4,32},{5,33},{6,34},{7,35},{8,64},{9,65},... | collective-permute-start | bytes 589832 | tf_op jit(solution)/shard_map/ppermute | solution.py:442
  52.6 20.7 %all-to-all-start = ((f32[8,64,256]{2,1,0:T(8,128)}), f32[8,64,256]{2,1,0:T(8,128)S(1)}, u32[]{:S(2)}, u32[]{:S(2)}) async-start(f32[8,64,256]{2,1,0:T(8,128)} %broadcast_in_dim.53), calls=%async_computation | async-start | bytes 1048576 | tf_op jit(solution)/shard_map/all_to_all | solution.py:367
  74.3 4.1 %collective-permute-start.22 = (f32[32,256]{1,0:T(8,128)S(1)}, f32[32,256]{1,0:T(8,128)S(1)}, u32[]{:S(2)}, u32[]{:S(2)}) collective-permute-start(f32[32,256]{1,0:T(8,128)S(1)} %constant_dynamic-slice_fusion), channel_id=1, source_target_pairs={{0,3},{1,0},{2,1},{3,2},{4,7},{5,4},{6,5},{7,6},{8,11},{9,8},{10,9... | collective-permute-start | bytes 98312 | tf_op jit(solution)/shard_map/ppermute | solution.py:376
  77.1 4.3 %collective-permute-start.21 = (f32[32,256]{1,0:T(8,128)S(1)}, f32[32,256]{1,0:T(8,128)S(1)}, u32[]{:S(2)}, u32[]{:S(2)}) collective-permute-start(f32[32,256]{1,0:T(8,128)S(1)} %constant_dynamic-slice_fusion), channel_id=1, source_target_pairs={{0,2},{1,3},{2,0},{3,1},{4,6},{5,7},{6,4},{7,5},{8,10},{9,11},{10,... | collective-permute-start | bytes 98312 | tf_op jit(solution)/shard_map/ppermute | solution.py:376
  77.5 4.3 %collective-permute-start.20 = (f32[32,256]{1,0:T(8,128)S(1)}, f32[32,256]{1,0:T(8,128)S(1)}, u32[]{:S(2)}, u32[]{:S(2)}) collective-permute-start(f32[32,256]{1,0:T(8,128)S(1)} %constant_dynamic-slice_fusion), channel_id=1, source_target_pairs={{0,1},{1,2},{2,3},{3,0},{4,5},{5,6},{6,7},{7,4},{8,9},{9,10},{10,1... | collective-permute-start | bytes 98312 | tf_op jit(solution)/shard_map/ppermute | solution.py:376
  81.7 7.7 %collective-permute-start.23 = (f32[32,256]{1,0:T(8,128)S(1)}, f32[32,256]{1,0:T(8,128)S(1)}, u32[]{:S(2)}, u32[]{:S(2)}) collective-permute-start(f32[32,256]{1,0:T(8,128)S(1)} %add_add_fusion.1), channel_id=1, source_target_pairs={{0,32},{32,0},{1,33},{33,1},{2,34},{34,2},{3,35},{35,3},{4,36},{36... | collective-permute-start | bytes 98312 | tf_op jit(solution)/shard_map/ppermute | solution.py:376
  89.5 7.3 %collective-permute-start.26 = (f32[32,256]{1,0:T(8,128)S(1)}, f32[32,256]{1,0:T(8,128)S(1)}, u32[]{:S(2)}, u32[]{:S(2)}) collective-permute-start(f32[32,256]{1,0:T(8,128)S(1)} %add.156), channel_id=1, source_target_pairs={{0,192},{64,0},{128,64},{192,128},{1,193},{65,1},{129,65},{193,129... | collective-permute-start | bytes 98312 | tf_op jit(solution)/shard_map/ppermute | solution.py:376
  91.5 6.5 %collective-permute-start.25 = (f32[32,256]{1,0:T(8,128)S(1)}, f32[32,256]{1,0:T(8,128)S(1)}, u32[]{:S(2)}, u32[]{:S(2)}) collective-permute-start(f32[32,256]{1,0:T(8,128)S(1)} %add.156), channel_id=1, source_target_pairs={{0,128},{64,192},{128,0},{192,64},{1,129},{65,193},{129,1},{193,65... | collective-permute-start | bytes 98312 | tf_op jit(solution)/shard_map/ppermute | solution.py:376
  93.4 4.7 %collective-permute-start.24 = (f32[32,256]{1,0:T(8,128)S(1)}, f32[32,256]{1,0:T(8,128)S(1)}, u32[]{:S(2)}, u32[]{:S(2)}) collective-permute-start(f32[32,256]{1,0:T(8,128)S(1)} %add.156), channel_id=1, source_target_pairs={{0,64},{64,128},{128,192},{192,0},{1,65},{65,129},{129,193},{193,1... | collective-permute-start | bytes 98312 | tf_op jit(solution)/shard_map/ppermute | solution.py:376
  93.4 11.3 %collective-permute-start.17 = (f32[64,512]{1,0:T(8,128)S(1)}, f32[64,512]{1,0:T(8,128)S(1)}, u32[]{:S(2)}, u32[]{:S(2)}) collective-permute-start(f32[64,512]{1,0:T(8,128)S(1)} %get-tuple-element.33), channel_id=1, source_target_pairs={{0,128},{64,192},{128,0},{192,64},{1,129},{65,193},{129,1},{193,65... | collective-permute-start | bytes 393224 | tf_op jit(solution)/shard_map/ppermute | solution.py:376
  95.4 9.4 %collective-permute-start.16 = (f32[64,512]{1,0:T(8,128)S(1)}, f32[64,512]{1,0:T(8,128)S(1)}, u32[]{:S(2)}, u32[]{:S(2)}) collective-permute-start(f32[64,512]{1,0:T(8,128)S(1)} %get-tuple-element.33), channel_id=1, source_target_pairs={{0,64},{64,128},{128,192},{192,0},{1,65},{65,129},{129,193},{193,1... | collective-permute-start | bytes 393224 | tf_op jit(solution)/shard_map/ppermute | solution.py:376
  96.7 8.0 %collective-permute-start.18 = (f32[64,512]{1,0:T(8,128)S(1)}, f32[64,512]{1,0:T(8,128)S(1)}, u32[]{:S(2)}, u32[]{:S(2)}) collective-permute-start(f32[64,512]{1,0:T(8,128)S(1)} %get-tuple-element.33), channel_id=1, source_target_pairs={{0,192},{64,0},{128,64},{192,128},{1,193},{65,1},{129,65},{193,129... | collective-permute-start | bytes 393224 | tf_op jit(solution)/shard_map/ppermute | solution.py:376
  98.8 15.4 %all-to-all-start.1 = ((f32[8,32,256]{2,1,0:T(8,128)}), f32[8,32,256]{2,1,0:T(8,128)S(1)}, u32[]{:S(2)}, u32[]{:S(2)}) async-start(f32[8,32,256]{2,1,0:T(8,128)} %broadcast_in_dim.55), calls=%async_computation.1 | async-start | bytes 524288 | tf_op jit(solution)/shard_map/all_to_all | solution.py:367
  105.6 9.6 %collective-permute-start.19 = (f32[4,64,512]{2,1,0:T(8,128)}, f32[4,64,512]{2,1,0:T(8,128)}, u32[]{:S(2)}, u32[]{:S(2)}) collective-permute-start(f32[4,64,512]{2,1,0:T(8,128)} %pad_maximum_fusion.cols_ref), channel_id=1, source_target_pairs={{0,32},{32,0},{1,33},{33,1},{2,34},{34,2},{3,35},{35,3},{4,36},{36... | collective-permute-start | bytes 1572872 | tf_op jit(solution)/shard_map/ppermute | solution.py:376
  110.4 13.7 %collective-permute-start.15 = (f32[512,256]{1,0:T(8,128)S(1)}, f32[512,256]{1,0:T(8,128)}, u32[]{:S(2)}, u32[]{:S(2)}) collective-permute-start(f32[512,256]{1,0:T(8,128)S(1)} %bitcast.56), channel_id=1, source_target_pairs={{0,3},{1,0},{2,1},{3,2},{4,7},{5,4},{6,5},{7,6},{8,11},{9,8},{10,9... | collective-permute-start | bytes 1572872 | tf_op jit(solution)/shard_map/ppermute | solution.py:376
  110.8 14.8 %collective-permute-start.14 = (f32[512,256]{1,0:T(8,128)S(1)}, f32[512,256]{1,0:T(8,128)}, u32[]{:S(2)}, u32[]{:S(2)}) collective-permute-start(f32[512,256]{1,0:T(8,128)S(1)} %bitcast.57), channel_id=1, source_target_pairs={{0,2},{1,3},{2,0},{3,1},{4,6},{5,7},{6,4},{7,5},{8,10},{9,11},{10,... | collective-permute-start | bytes 1572872 | tf_op jit(solution)/shard_map/ppermute | solution.py:376
  112.0 25.5 %collective-permute-start.13 = (f32[512,256]{1,0:T(8,128)S(1)}, f32[512,256]{1,0:T(8,128)}, u32[]{:S(2)}, u32[]{:S(2)}) collective-permute-start(f32[512,256]{1,0:T(8,128)S(1)} %bitcast.58), channel_id=1, source_target_pairs={{0,1},{1,2},{2,3},{3,0},{4,5},{5,6},{6,7},{7,4},{8,9},{9,10},{10,1... | collective-permute-start | bytes 1572872 | tf_op jit(solution)/shard_map/ppermute | solution.py:376
  115.2 22.3 %copy-start = (f32[2048,512]{1,0:T(8,128)S(1)}, f32[2048,512]{1,0:T(8,128)}, u32[]{:S(2)}) copy-start(f32[2048,512]{1,0:T(8,128)} %trailing_ref.3) | copy-start | bytes 12582916
